TPU v7x, 32 devices: a whole 2x2x4 slice. The times are simulated.
32 devices in a mesh: dp: 4 (over x, core), ep: 8 (over z, y).
Axes of the slice: x: 2, y: 2, z: 4, core: 2. Of those that a mesh axis runs over, the one named last changes fastest.
Arguments:
- tokens: bfloat16 [4096, 7168], P(('dp', 'ep')), may hold values from -6 to 6
- out_grad: bfloat16 [4096, 7168], P(('dp', 'ep')), may hold values from -3 to 3
- expert_ids: int32 [4096, 8], P(('dp', 'ep')), may hold values from 0 to 255, as said below
- route_weights: bfloat16 [4096, 8], P(('dp', 'ep')), may hold values from 0.099609375 to 1
- gate_matrix: bfloat16 [7168, 2048], P('dp', 'ep'), may hold values from -0.0625 to 0.0625
- up_matrix: bfloat16 [7168, 2048], P('dp', 'ep'), may hold values from -0.0625 to 0.0625
- down_matrix: bfloat16 [7168, 2048], P('dp', 'ep'), may hold values from -0.125 to 0.125
Outputs:
- input_gradient: bfloat16 [4096, 7168], P(('dp', 'ep'))
- route_gradient: float32 [4096, 8], P(('dp', 'ep'))
- gate_gradient: bfloat16 [7168, 2048], P('dp', 'ep')
- up_gradient: bfloat16 [7168, 2048], P('dp', 'ep')
- down_gradient: bfloat16 [7168, 2048], P('dp', 'ep')
Inputs may be any that keep to these rules, and one draw needn't show every extreme that they name: `expert_ids`: each row names 8 different ids, 2 in each of 4 groups of 32 consecutive ids. In each aligned block of 1024 rows, one id that is a multiple of 256 is named by 8 or more rows of every aligned block of 128 rows inside it.
All inputs are finite; a program needn't handle non-finite values.
Results may differ from a plain program's by a relative error of at most 0.014.
Values may be sent and summed in bfloat16 or wider, within the bound.
A program may use at most 128 MiB of HBM per device.

v0:
```python
import functools
import jax
import jax.numpy as jnp
from jax import lax
from jax.experimental import pallas as pl
from jax.experimental.pallas import tpu as pltpu
from jax.sharding import PartitionSpec as P

ROUTED = 256
TOPK = 8
SLICES = 8
CAP = 8
LANES = 128
BF = jnp.bfloat16
F32 = jnp.float32
MESH = pl.DeviceIdType.MESH


def kernel(
    n_dp, n_ep,
    tok_hbm, grad_hbm, ids_ref, rw_ref, a_hbm, b_hbm, c_hbm,
    fin, sel_ref, ga_hbm, gb_hbm, gc_hbm,
    tokbuf, gradbuf, wab, wc, send1, shard, ag, xs, ys, gates, psum, arsend, arrecv,
    deltas, scaleds, rp, r1recv, r2send, r2recv, retbuf, ga, gb, gc,
    in_sem, w_sem, s1s, s1r, s2s, s2d, s2r, sas, s3s, s3r, ars, arr, r1s, r1r, r2s, r2r, fs, fr,
):
    experts = n_ep // SLICES
    stride = ROUTED // experts
    places = experts * CAP
    n_hi = n_ep // 2
    rows, width = tok_hbm.shape
    lw, hid = a_hbm.shape
    nb = n_dp.bit_length() - 1
    chunk = 2 * n_dp * CAP
    half = n_dp * CAP
    g = lax.axis_index("dp")
    e = lax.axis_index("ep")
    hi, lo = e // 2, e % 2
    other = hi * 2 + (1 - lo)
    mine_w = e // SLICES

    def rc(src, dst, ss, rs, **where):
        return pltpu.make_async_remote_copy(
            src_ref=src, dst_ref=dst, send_sem=ss, recv_sem=rs,
            device_id=where, device_id_type=MESH)

    def cols(j):
        gp = lax.rem(g + j, n_dp)
        return gp, pl.ds(pl.multiple_of(gp * lw, LANES), lw)

    order = [n_dp // 2] + [j for j in range(1, n_dp) if j != n_dp // 2] + [0]
    loads = []
    for q, (src, buf) in enumerate(((tok_hbm, tokbuf), (grad_hbm, gradbuf))):
        for j in order:
            gp, ds = cols(j)
            c = pltpu.make_async_copy(src.at[:, ds], buf.at[j], in_sem.at[q, j])
            c.start()
            loads.append((q, j, gp, buf, c))
    wloads = [
        pltpu.make_async_copy(a_hbm, wab.at[:, pl.ds(0, hid)], w_sem.at[0]),
        pltpu.make_async_copy(b_hbm, wab.at[:, pl.ds(hid, hid)], w_sem.at[1]),
        pltpu.make_async_copy(c_hbm, wc, w_sem.at[2]),
    ]

    barrier = pltpu.get_barrier_semaphore()
    for j in range(1, n_dp):
        pl.semaphore_signal(barrier, inc=1, device_id={"dp": lax.rem(g + j, n_dp)}, device_id_type=MESH)
    for j in range(1, n_hi):
        pl.semaphore_signal(
            barrier, inc=1, device_id={"ep": lax.rem(hi + j, n_hi) * 2 + lo}, device_id_type=MESH)
    pl.semaphore_signal(barrier, inc=1, device_id={"ep": other}, device_id_type=MESH)

    pad = jnp.zeros((LANES - TOPK, rows), F32)
    ids = jnp.concatenate([ids_ref[...].astype(F32), pad], axis=0).T
    rw = jnp.concatenate([rw_ref[...].astype(F32), pad], axis=0).T
    lane = lax.broadcasted_iota(jnp.int32, (rows, LANES), 1)
    wanted = jnp.where(lane < places, (lane // CAP) * stride, -1).astype(F32)
    hits = jnp.zeros((rows, LANES), F32)
    wts = jnp.zeros((rows, LANES), F32)
    for k in range(TOPK):
        m = ids[:, k:k + 1] == wanted
        hits = hits + jnp.where(m, 1.0, 0.0)
        wts = wts + jnp.where(m, rw[:, k:k + 1], 0.0)
    tr = lax.broadcasted_iota(jnp.int32, (rows, rows), 0)
    tc = lax.broadcasted_iota(jnp.int32, (rows, rows), 1)
    lower = jnp.where(tc < tr, 1.0, 0.0).astype(BF)
    slot = jnp.dot(lower, hits.astype(BF), preferred_element_type=F32)
    sel = jnp.where(slot == (lane % CAP).astype(F32), hits, 0.0)
    sel_ref[...] = sel
    selT = sel.T[:places].astype(BF)
    gwT = (sel * wts).T[:places].astype(BF)
    gate = jnp.dot(gwT, jnp.ones((rows, LANES), BF), preferred_element_type=F32)
    gate = gate.reshape(experts, CAP, LANES).astype(BF)

    pl.semaphore_wait(barrier, n_dp - 1 + n_hi)

    pieces = (pl.ds(0, lw), pl.ds(lw, lw + LANES))

    def slices(j, q, gp):
        return rc(send1.at[j, :, :, pieces[q]], shard.at[:, g, :, pieces[q]], s1s.at[q, j], s1r.at[q, g], dp=gp)

    for q, j, gp, buf, c in loads:
        c.wait()
        r = jnp.dot(selT, buf[j], preferred_element_type=F32).reshape(experts, CAP, lw).astype(BF)
        if j:
            send1[j, :, :, q * lw:(q + 1) * lw] = r
            if q:
                send1[j, :, :, 2 * lw:] = gate
            slices(j, q, gp).start()
        else:
            shard[:, g, :, q * lw:(q + 1) * lw] = r
            if q:
                shard[:, g, :, 2 * lw:] = gate
    for c in wloads:
        c.start()

    per = SLICES // 2
    pos = hi % per
    base = hi - pos

    def at_order(k):
        m = jnp.where(pos < per - 1 - pos, pos, per - 1 - pos)
        near = jnp.where(k % 2 == 1, pos - (k + 1) // 2, pos + k // 2)
        far = jnp.where(pos < per - 1 - pos, k, per - 1 - k)
        return jnp.where(k <= 2 * m, near, far)

    def seen(h, q):
        return ag.at[h * 2 + lo, :, :, pieces[q]]

    def link(p, v, q, up):
        h = v * per + p
        to = hi + 1 - 2 * up
        return rc(seen(h, q), seen(h, q), (s2d if up else s2s).at[h, q], s2r.at[h, q], ep=to * 2 + lo)

    def link_in(p, v, q):
        h = v * per + p
        return rc(seen(h, q), seen(h, q), s2s.at[h, q], s2r.at[h, q], ep=other)

    def fwd(p, v, q):
        h = v * per + p
        return rc(seen(h, q), seen(h, q), s3s.at[h, q], s3r.at[h, q], ep=other)

    def fwd_in(p, v, q):
        h = v * per + p
        r = ag.at[h * 2 + 1 - lo, :, :, pieces[q]]
        return rc(r, r, s3s.at[h, q], s3r.at[h, q], ep=other)

    def across(i, q):
        h = lax.rem(hi + i * per, n_hi)
        return rc(shard.at[h // per, :, :, pieces[q]], seen(hi, q), sas.at[i, q], s2r.at[hi, q], ep=h * 2 + lo)

    def across_in(i, q):
        h = lax.rem(hi + i * per, n_hi)
        return rc(seen(h, q), seen(h, q), sas.at[i, q], s2r.at[h, q], ep=other)

    def onward(p, v, q, wait):
        @pl.when((p <= pos) & (pos < per - 1))
        def _():
            d = link(p, v, q, 0)
            d.wait_send() if wait else d.start()

        @pl.when((p >= pos) & (pos > 0))
        def _():
            d = link(p, v, q, 1)
            d.wait_send() if wait else d.start()

    for q in range(2):
        for j in range(1, n_dp):
            src = lax.rem(g + j, n_dp)
            rc(send1.at[j, :, :, pieces[q]], shard.at[:, src, :, pieces[q]], s1s.at[q, j], s1r.at[q, src], dp=src).wait_recv()
        for i in range(1, experts):
            across(i, q).start()
        if q:
            ag[e, :, :, lw:] = shard[mine_w, :, :, lw:]
        else:
            ag[e, :, :, :lw] = shard[mine_w, :, :, :lw]
        onward(pos, mine_w, q, False)
        fwd(pos, mine_w, q).start()
        for i in range(1, experts):
            across_in(i, q).wait_recv()
            v = lax.rem(mine_w + i, experts)
            onward(pos, v, q, False)
            fwd(pos, v, q).start()
    for c in wloads:
        c.wait()

    def ar(b, h):
        bit = 1 << b
        peer = g + (1 - 2 * ((g // bit) % 2)) * bit
        return rc(arsend.at[b, h], arrecv.at[b, h], ars.at[b, h], arr.at[b, h], dp=peer)

    def at_chunk(h):
        return pl.ds(pl.multiple_of(h * chunk, 16), chunk)

    def r1(h):
        return rc(rp.at[h, 1 - lo], r1recv.at[h], r1s.at[h], r1r.at[h], ep=other)

    def chunk_of(t):
        p, v = at_order(t // experts), t % experts
        return p, v, v * per + p

    def finish(i):
        p, v, h = chunk_of(i)
        ar(nb - 1, h).wait_recv()
        s = psum[h] + arrecv[nb - 1, h].astype(F32)
        gate_pre, up_pre, proj = s[:, :hid], s[:, hid:2 * hid], s[:, 2 * hid:]
        scaling = gates[at_chunk(h), 0:1]
        sig = 1.0 / (1.0 + jnp.exp(-gate_pre))
        sw = gate_pre * sig
        hidden = (sw * up_pre).astype(BF).astype(F32)
        route = jnp.sum(hidden * proj, axis=1, keepdims=True)
        gh = scaling * proj
        d1 = (gh * up_pre * sig * (1.0 + gate_pre * (1.0 - sig))).astype(BF)
        d2 = (gh * sw).astype(BF)
        deltas[at_chunk(h), 0:hid] = d1
        deltas[at_chunk(h), hid:] = d2
        scaleds[at_chunk(h), :] = (scaling * hidden).astype(BF)
        part = lax.dot_general(
            jnp.concatenate([d1, d2], axis=1), wab[...], (((1,), (1,)), ((), ())),
            preferred_element_type=F32)
        rp[h, :, :, 0:lw] = part.reshape(2, half, lw).astype(BF)
        rp[h, :, :, lw:] = jnp.broadcast_to(route, (chunk, LANES)).reshape(2, half, LANES).astype(BF)
        r1(h).start()

    def flow(t, carry):
        @pl.when((t >= experts) & (t < n_hi))
        def _():
            p, v, h = chunk_of(t)
            for q in range(2):
                link_in(p, v, q).wait_recv()
                onward(p, v, q, False)
                fwd(p, v, q).start()

        @pl.when((t >= 2) & (t <= n_hi + 1))
        def _():
            p, v, h = chunk_of(t - 2)
            fwd_in(p, v, 0).wait_recv()
            x = ag[pl.ds(h * 2, 2), :, :, 0:lw].astype(F32).reshape(chunk, lw).astype(BF)
            xs[at_chunk(h), :] = x
            p1 = jnp.dot(x, wab[...], preferred_element_type=F32)
            psum[h, :, 0:2 * hid] = p1
            arsend[0, h, :, 0:2 * hid] = p1.astype(BF)
            fwd_in(p, v, 1).wait_recv()
            y = ag[pl.ds(h * 2, 2), :, :, lw:2 * lw].astype(F32).reshape(chunk, lw).astype(BF)
            gates[at_chunk(h), :] = ag[pl.ds(h * 2, 2), :, :, 2 * lw:].astype(F32).reshape(chunk, LANES)
            ys[at_chunk(h), :] = y
            p2 = jnp.dot(y, wc[...], preferred_element_type=F32)
            psum[h, :, 2 * hid:] = p2
            arsend[0, h, :, 2 * hid:] = p2.astype(BF)
            ar(0, h).start()

        for b in range(nb - 1):
            @pl.when((t >= 3 + b) & (t < n_hi + 3 + b))
            def _(b=b):
                p, v, h = chunk_of(t - 3 - b)
                ar(b, h).wait_recv()
                s = psum[h] + arrecv[b, h].astype(F32)
                psum[h] = s
                arsend[b + 1, h] = s.astype(BF)
                ar(b + 1, h).start()

        @pl.when(t >= nb + 2)
        def _():
            finish(t - nb - 2)
        return carry

    lax.fori_loop(0, n_hi + nb + 2, flow, 0)

    def r2(h):
        return rc(r2send.at[h], r2recv.at[hi], r2s.at[h], r2r.at[hi], ep=h * 2 + lo)

    def pair(h):
        r1(h).wait_recv()
        return rp[h, lo].astype(F32) + r1recv[h].astype(F32)

    def combine(t, carry):
        p, v, h = chunk_of(t)
        both = pair(h).astype(BF)

        @pl.when(h != hi)
        def _():
            r2send[h] = both
            r2(h).start()

        @pl.when(h == hi)
        def _():
            r2recv[hi] = both
        return carry

    lax.fori_loop(0, n_hi, combine, 0)

    tile = 256 if lw % 256 == 0 else 128

    def wgrad(i, carry):
        ds = pl.ds(pl.multiple_of(i * tile, LANES), tile)
        dn = (((0,), (0,)), ((), ()))
        both = lax.dot_general(xs[:, ds], deltas[...], dn, preferred_element_type=F32).astype(BF)
        ga[ds, :] = both[:, :hid]
        gb[ds, :] = both[:, hid:]
        gc[ds, :] = lax.dot_general(ys[:, ds], scaleds[...], dn, preferred_element_type=F32).astype(BF)
        return carry

    lax.fori_loop(0, lw // tile, wgrad, 0)
    outs = [
        pltpu.make_async_copy(ga, ga_hbm, w_sem.at[0]),
        pltpu.make_async_copy(gb, gb_hbm, w_sem.at[1]),
        pltpu.make_async_copy(gc, gc_hbm, w_sem.at[2]),
    ]
    for c in outs:
        c.start()

    for i in range(1, n_hi):
        h = lax.rem(hi + i, n_hi)
        rc(r2send.at[h], r2recv.at[h], r2s.at[h], r2r.at[h], ep=h * 2 + lo).wait_recv()
    for w in range(experts):
        acc = r2recv[w * per].astype(F32)
        for j in range(1, per):
            acc = acc + r2recv[w * per + j].astype(F32)
        retbuf[:, w] = acc.reshape(n_dp, CAP, lw + LANES).astype(BF)
    for j in range(1, n_dp):
        gp = lax.rem(g + j, n_dp)
        rc(retbuf.at[gp], fin.at[g], fs.at[j], fr.at[g], dp=gp).start()
    fin[g] = retbuf[g]
    for j in range(1, n_dp):
        gp = lax.rem(g + j, n_dp)
        rc(retbuf.at[gp], fin.at[gp], fs.at[j], fr.at[gp], dp=gp).wait_recv()

    for j in range(1, n_dp):
        gp = lax.rem(g + j, n_dp)
        slices(j, 0, gp).wait_send()
        slices(j, 1, gp).wait_send()
        rc(retbuf.at[gp], fin.at[g], fs.at[j], fr.at[g], dp=gp).wait_send()

    def drain(i, carry):
        h = lax.rem(hi + i, n_hi)
        for q in range(2):
            fwd(h % per, h // per, q).wait_send()
            onward(h % per, h // per, q, True)
        for b in range(nb):
            ar(b, h).wait_send()
        r1(h).wait_send()

        @pl.when(i >= 1)
        def _():
            r2(h).wait_send()
        return carry

    lax.fori_loop(0, n_hi, drain, 0)
    for i in range(1, experts):
        for q in range(2):
            across(i, q).wait_send()
    for c in outs:
        c.wait()


def finish_kernel(
    fin, sel_ref, ids_ref, ga_in, gb_in, gc_in, ig_hbm, rg_ref, ga_out, gb_out, gc_out,
    buf, obuf, sem_in, sem_out, osem,
):
    n_dp, experts, _, wide = fin.shape
    places = experts * CAP
    lw = wide - LANES
    rows = sel_ref.shape[0]
    stride = ROUTED // experts
    ins = [pltpu.make_async_copy(r, buf.at[i], sem_in.at[i]) for i, r in enumerate((ga_in, gb_in, gc_in))]
    outs = [pltpu.make_async_copy(buf.at[i], r, sem_out.at[i]) for i, r in enumerate((ga_out, gb_out, gc_out))]
    for c in ins:
        c.start()
    sel = sel_ref[...]
    selP = sel[:, :places].astype(BF)
    for c, o in zip(ins, outs):
        c.wait()
        o.start()
    ocopies = []
    for j in range(n_dp):
        vals = fin[j].astype(F32).reshape(places, wide)
        obuf[:, j * lw:(j + 1) * lw] = jnp.dot(
            selP, vals[:, :lw].astype(BF), preferred_element_type=F32).astype(BF)
        ds = pl.ds(j * lw, lw)
        c = pltpu.make_async_copy(obuf.at[:, ds], ig_hbm.at[:, ds], osem.at[j])
        c.start()
        ocopies.append(c)
    vals = fin[0].astype(F32).reshape(places, wide)
    route = jnp.concatenate([vals[:, lw:], jnp.zeros((LANES - places, LANES), F32)], axis=0).T[0:1]
    terms = sel * route
    pad = jnp.zeros((LANES - TOPK, rows), F32)
    ids = jnp.concatenate([ids_ref[...].astype(F32), pad], axis=0).T
    lane = lax.broadcasted_iota(jnp.int32, (rows, LANES), 1)
    wanted = jnp.where(lane < places, (lane // CAP) * stride, -1).astype(F32)
    rg = jnp.zeros((rows, LANES), F32)
    for k in range(TOPK):
        v = jnp.sum(jnp.where(ids[:, k:k + 1] == wanted, terms, 0.0), axis=1, keepdims=True)
        rg = jnp.where(lane == k, v, rg)
    rg_ref[...] = rg.T[:TOPK]
    for c in outs + ocopies:
        c.wait()


def body(tokens, out_grad, expert_ids, route_weights, gate_matrix, up_matrix, down_matrix):
    n_dp, n_ep = lax.axis_size("dp"), lax.axis_size("ep")
    experts = n_ep // SLICES
    n_hi = n_ep // 2
    rows, width = tokens.shape
    lw, hid = gate_matrix.shape
    nb = n_dp.bit_length() - 1
    chunk = 2 * n_dp * CAP
    half = n_dp * CAP
    total = n_hi * chunk
    C = 2 * lw + LANES
    R = lw + LANES
    V = pltpu.VMEM
    D = lambda *s: pltpu.SemaphoreType.DMA(s)
    anyspec = pl.BlockSpec(memory_space=pl.ANY)
    vspec = pl.BlockSpec(memory_space=pltpu.VMEM)
    ids = expert_ids.T
    grad = jax.ShapeDtypeStruct((lw, hid), BF)
    fin, sel, ga, gb, gc = pl.pallas_call(
        functools.partial(kernel, n_dp, n_ep),
        out_shape=(
            jax.ShapeDtypeStruct((n_dp, experts, CAP, R), BF),
            jax.ShapeDtypeStruct((rows, LANES), F32),
            grad, grad, grad,
        ),
        in_specs=[anyspec, anyspec, vspec, vspec, anyspec, anyspec, anyspec],
        out_specs=(vspec, vspec, anyspec, anyspec, anyspec),
        scratch_shapes=[
            V((n_dp, rows, lw), BF), V((n_dp, rows, lw), BF), V((lw, 2 * hid), BF), V((lw, hid), BF),
            V((n_dp, experts, CAP, C), BF), V((experts, n_dp, CAP, C), BF), V((n_ep, n_dp, CAP, C), BF),
            V((total, lw), BF), V((total, lw), BF), V((total, LANES), F32),
            V((n_hi, chunk, 3 * hid), F32), V((nb, n_hi, chunk, 3 * hid), BF), V((nb, n_hi, chunk, 3 * hid), BF),
            V((total, 2 * hid), BF), V((total, hid), BF),
            V((n_hi, 2, half, R), BF), V((n_hi, half, R), BF), V((n_hi, half, R), BF), V((n_hi, half, R), BF),
            V((n_dp, experts, CAP, R), BF),
            V((lw, hid), BF), V((lw, hid), BF), V((lw, hid), BF),
            D(2, n_dp), D(3), D(2, n_dp), D(2, n_dp), D(n_hi, 2), D(n_hi, 2), D(n_hi, 2), D(experts, 2),
            D(n_hi, 2), D(n_hi, 2),
            D(nb, n_hi), D(nb, n_hi), D(n_hi), D(n_hi), D(n_hi), D(n_hi), D(n_dp), D(n_dp),
        ],
        compiler_params=pltpu.CompilerParams(
            collective_id=0, has_side_effects=True, vmem_limit_bytes=67043328),
    )(tokens, out_grad, ids, route_weights.T, gate_matrix, up_matrix, down_matrix)
    ig, rg, ga, gb, gc = pl.pallas_call(
        finish_kernel,
        out_shape=(
            jax.ShapeDtypeStruct((rows, width), BF),
            jax.ShapeDtypeStruct((TOPK, rows), F32),
            grad, grad, grad,
        ),
        in_specs=[vspec, vspec, vspec, anyspec, anyspec, anyspec],
        out_specs=(anyspec, vspec, anyspec, anyspec, anyspec),
        scratch_shapes=[V((3, lw, hid), BF), V((rows, width), BF), D(3), D(3), D(n_dp)],
        compiler_params=pltpu.CompilerParams(vmem_limit_bytes=67043328),
    )(fin, sel, ids, ga, gb, gc)
    return ig, rg.T, ga, gb, gc


def solution(mesh):
    return jax.shard_map(
        body,
        mesh=mesh,
        in_specs=(
            P(("dp", "ep"), None),
            P(("dp", "ep"), None),
            P(("dp", "ep"), None),
            P(("dp", "ep"), None),
            P("dp", "ep"),
            P("dp", "ep"),
            P("dp", "ep"),
        ),
        out_specs=(
            P(("dp", "ep"), None),
            P(("dp", "ep"), None),
            P("dp", "ep"),
            P("dp", "ep"),
            P("dp", "ep"),
        ),
        check_vma=False,
    )
```

profile of v0, /device:TPU:0, one launch (start us, length us, event | category | flops | bytes accessed | tf_op | source)
XLA Modules:
  0.0 62.6 jit_solution(5973473463302796960)
XLA Ops:
  0.6 56.9 %shard_map.110 = (bf16[4,1,8,1920]{3,2,1,0:T(8,128)(2,1)}, f32[128,128]{1,0:T(8,128)}, bf16[1792,256]{1,0:T(8,128)(2,1)}, bf16[1792,256]{1,0:T(8,128)(2,1)}, bf16[1792,256]{1,0:T(8,128)(2,1)}) custom-call(bf16[128,7168]{1,0:T(8,128)(2,1)} %tok_hbm.1, bf16[128,7168]{1,0:T(8,128)(2,1)} %grad_hbm.1, s32[8,128]{1,0:T(8,128)} %bitcast.3, bf16[8,128]{1,0:T(8,128)(2,1)} %bitcast.5, ...), custom_call_target="tpu_custom_call" | custom-call | tf_op jit(solution)/shard_map/pallas_call | solution.py:417
  57.5 5.1 %shard_map.111 = (bf16[128,7168]{1,0:T(8,128)(2,1)}, f32[8,128]{1,0:T(8,128)}, bf16[1792,256]{1,0:T(8,128)(2,1)}, bf16[1792,256]{1,0:T(8,128)(2,1)}, bf16[1792,256]{1,0:T(8,128)(2,1)}) custom-call(bf16[4,1,8,1920]{3,2,1,0:T(8,128)(2,1)} %get-tuple-element.15.fin, f32[128,128]{1,0:T(8,128)} %get-tuple-element.16.sel_ref, s32[8,128]{1,0:T(8,128)} %bitcast.4, ...), custom_call_target="tpu_custom_call" | custom-call | tf_op jit(solution)/shard_map/pallas_call | solution.py:442
where the time goes:
time: 62.8 us; the launch traced here: 62.6 us
  Pallas kernels  61.9 us (99%)
  between operations  0.64 us (1%)
    pallas_call x1, Pallas kernels, body(): pl.pallas_call(functools.partial(kernel, n_dp, n_ep), out_shape=(jax.Shap...  56.9 us
    pallas_call x1, Pallas kernels, body(): pl.pallas_call(finish_kernel, out_shape=(jax.ShapeDtypeStruct((rows, widt...  5.06 us

commit v1 on v0

v1 whole, which is shorter than its diff:
```python
import functools
import jax
import jax.numpy as jnp
from jax import lax
from jax.experimental import pallas as pl
from jax.experimental.pallas import tpu as pltpu
from jax.sharding import PartitionSpec as P

ROUTED = 256
TOPK = 8
SLICES = 8
CAP = 8
LANES = 128
PAIR = 2 * CAP
VMEM_BYTES = 56 * 1024 * 1024
BF = jnp.bfloat16
F32 = jnp.float32
MESH = pl.DeviceIdType.MESH


def kernel(
    n_dp, n_ep,
    tok_hbm, grad_hbm, ids_hbm, rw_hbm, a_hbm, b_hbm, c_hbm,
    ret, sel_ref, ga, gb, gc,
    ids_buf, rw_buf, tokbuf, gradbuf, wab, wc, send1, shard, xs, ys,
    psx, psy, asx, arx, asy, ary, deltas, hiddens, rp, r1recv, r2send,
    in_sem, id_sem, w_sem, s1s, s1r, sus, sds, slr, sfs, sfr, ars, arr, r1s, r1r, r2s, r2r,
):
    experts = n_ep // SLICES
    stride = ROUTED // experts
    places = experts * CAP
    n_hi = n_ep // 2
    per = SLICES // 2
    n_pair = n_dp // 2
    rows, width = tok_hbm.shape
    lw, hid = a_hbm.shape
    nb = n_dp.bit_length() - 1
    chunk = 2 * n_dp * CAP
    half = n_dp * CAP
    g = lax.axis_index("dp")
    e = lax.axis_index("ep")
    hi, lo = e // 2, e % 2
    other = hi * 2 + (1 - lo)
    mine_w = hi // per
    pos = hi % per

    def rc(src, dst, ss, rs, **where):
        return pltpu.make_async_remote_copy(
            src_ref=src, dst_ref=dst, send_sem=ss, recv_sem=rs,
            device_id=where, device_id_type=MESH)

    def flip(j):
        gp = g
        for b in range(nb):
            if j >> b & 1:
                gp = gp + (1 - 2 * ((g // (1 << b)) % 2)) * (1 << b)
        return gp

    def line(i):
        return lax.rem(mine_w + i, experts)

    def place(v):
        return (v * per + pos) * 2 + lo

    id_copies = [
        pltpu.make_async_copy(ids_hbm, ids_buf, id_sem.at[0]),
        pltpu.make_async_copy(rw_hbm, rw_buf, id_sem.at[1]),
    ]
    for c in id_copies:
        c.start()
    order = list(range(1, n_dp)) + [0]
    loads = []
    for q, (src, buf) in enumerate(((tok_hbm, tokbuf), (grad_hbm, gradbuf))):
        for j in order:
            gp = flip(j)
            ds = pl.ds(pl.multiple_of(gp * lw, LANES), lw)
            c = pltpu.make_async_copy(src.at[:, ds], buf.at[j], in_sem.at[q, j])
            c.start()
            loads.append((q, j, gp, buf, c))
    wloads = [
        pltpu.make_async_copy(a_hbm, wab.at[:, pl.ds(0, hid)], w_sem.at[0]),
        pltpu.make_async_copy(b_hbm, wab.at[:, pl.ds(hid, hid)], w_sem.at[1]),
        pltpu.make_async_copy(c_hbm, wc, w_sem.at[2]),
    ]

    barrier = pltpu.get_barrier_semaphore()
    peers = 0
    for i in range(experts):
        for j in range(n_dp):
            if i or j:
                pl.semaphore_signal(
                    barrier, inc=1, device_id={"dp": flip(j), "ep": place(line(i))}, device_id_type=MESH)
                peers += 1
    pl.semaphore_signal(barrier, inc=1, device_id={"ep": other}, device_id_type=MESH)
    peers += 1

    @pl.when(pos > 0)
    def _():
        pl.semaphore_signal(barrier, inc=1, device_id={"ep": e - 2}, device_id_type=MESH)

    @pl.when(pos < per - 1)
    def _():
        pl.semaphore_signal(barrier, inc=1, device_id={"ep": e + 2}, device_id_type=MESH)

    for c in id_copies:
        c.wait()
    pad = jnp.zeros((LANES - TOPK, rows), F32)
    ids = jnp.concatenate([ids_buf[...].astype(F32), pad], axis=0).T
    rw = jnp.concatenate([rw_buf[...].astype(F32), pad], axis=0).T
    lane = lax.broadcasted_iota(jnp.int32, (rows, LANES), 1)
    wanted = jnp.where(lane < places, (lane // CAP) * stride, -1).astype(F32)
    hits = jnp.zeros((rows, LANES), F32)
    wts = jnp.zeros((rows, LANES), F32)
    for k in range(TOPK):
        m = ids[:, k:k + 1] == wanted
        hits = hits + jnp.where(m, 1.0, 0.0)
        wts = wts + jnp.where(m, rw[:, k:k + 1], 0.0)
    tr = lax.broadcasted_iota(jnp.int32, (rows, rows), 0)
    tc = lax.broadcasted_iota(jnp.int32, (rows, rows), 1)
    lower = jnp.where(tc < tr, 1.0, 0.0).astype(BF)
    slot = jnp.dot(lower, hits.astype(BF), preferred_element_type=F32)
    sel = jnp.where(slot == (lane % CAP).astype(F32), hits, 0.0)
    sel_ref[...] = sel
    picks = (sel.T[:places].astype(BF), (sel * wts).T[:places].astype(BF))

    pieces = (pl.ds(0, lw), pl.ds(lw, lw))

    def to_shard(j, i, q, gp):
        v = line(i)
        return rc(send1.at[j, v, :, pieces[q]], shard.at[mine_w, g, :, pieces[q]],
                  s1s.at[q, j, i], s1r.at[q, mine_w, g], dp=gp, ep=place(v))

    def shard_in(q, v, src):
        r = shard.at[v, src, :, pieces[q]]
        return rc(r, r, s1r.at[q, v, src], s1r.at[q, v, src], ep=other)

    first = True
    for q, j, gp, buf, c in loads:
        c.wait()
        r = jnp.dot(picks[q], buf[j], preferred_element_type=F32).reshape(experts, CAP, lw).astype(BF)
        send1[j, :, :, q * lw:(q + 1) * lw] = r
        if first:
            pl.semaphore_wait(
                barrier, peers + jnp.where(pos > 0, 1, 0) + jnp.where(pos < per - 1, 1, 0))
            first = False
        for i in range(experts):
            if i or j:
                to_shard(j, i, q, gp).start()
        if j == 0:
            if experts == 1:
                shard[0, g, :, q * lw:(q + 1) * lw] = r[0]
            else:
                shard[mine_w, g, :, q * lw:(q + 1) * lw] = send1[0, mine_w, :, q * lw:(q + 1) * lw]
    for c in wloads:
        c.start()

    def at_order(k):
        m = jnp.where(pos < per - 1 - pos, pos, per - 1 - pos)
        near = jnp.where(k % 2 == 1, pos - (k + 1) // 2, pos + k // 2)
        far = jnp.where(pos < per - 1 - pos, k, per - 1 - k)
        return jnp.where(k <= 2 * m, near, far)

    def rows_at(h, l, c):
        return pl.ds(pl.multiple_of(((h * 2 + l) * n_dp + 2 * c) * CAP, PAIR), PAIR)

    def piece(q, h, l, c):
        return (ys if q else xs).at[rows_at(h, l, c), :]

    def pair_at(ci):
        return lax.rem(g // 2 + ci, n_pair)

    def link(h, q, c, up):
        k = q * n_pair + c
        r = piece(q, h, lo, c)
        to = e + 2 - 4 * up
        return rc(r, r, (sds if up else sus).at[h, k], slr.at[h, k], ep=to)

    def link_in(h, q, c):
        k = q * n_pair + c
        r = piece(q, h, lo, c)
        return rc(r, r, slr.at[h, k], slr.at[h, k], ep=other)

    def fwd(h, q, c):
        k = q * n_pair + c
        r = piece(q, h, lo, c)
        return rc(r, r, sfs.at[h, k], sfr.at[h, k], ep=other)

    def fwd_in(h, q, c):
        k = q * n_pair + c
        r = piece(q, h, 1 - lo, c)
        return rc(r, r, sfr.at[h, k], sfr.at[h, k], ep=other)

    def onward(h, q, c, up, wait):
        @pl.when((pos > 0) if up else (pos < per - 1))
        def _():
            d = link(h, q, c, up)
            d.wait_send() if wait else d.start()

    for ci in range(n_pair):
        c = pair_at(ci)
        for q in range(2):
            for i in range(experts):
                v = line(i)
                h = v * per + pos
                for b in range(2):
                    src = flip(b) if ci == 0 else 2 * c + b
                    if not (ci == 0 and b == 0 and i == 0):
                        shard_in(q, v, src).wait_recv()
                both = shard[v, pl.ds(2 * c, 2), :, q * lw:(q + 1) * lw]
                (ys if q else xs)[rows_at(h, lo, c), :] = both.astype(F32).reshape(PAIR, lw).astype(BF)
                onward(h, q, c, 0, False)
                onward(h, q, c, 1, False)
                fwd(h, q, c).start()
    for c in wloads:
        c.wait()

    def ar(b, h, part):
        bit = 1 << b
        peer = g + (1 - 2 * ((g // bit) % 2)) * bit
        src, dst = ((asx, arx), (asy, ary))[part]
        return rc(src.at[b, h], dst.at[b, h], ars.at[b, h, part], arr.at[b, h, part], dp=peer)

    def at_chunk(h):
        return pl.ds(pl.multiple_of(h * chunk, PAIR), chunk)

    def r1(h):
        return rc(rp.at[h, 1 - lo], r1recv.at[h], r1s.at[h], r1r.at[h], ep=other)

    def chunk_of(t):
        return at_order(t // experts), t % experts

    def index_of(t):
        p, v = chunk_of(t)
        return v * per + p

    def gather_step(s):
        def one(v, carry):
            for q in range(2):
                for ci in range(n_pair):
                    c = pair_at(ci)

                    @pl.when(pos >= s)
                    def _():
                        h = v * per + pos - s
                        link_in(h, q, c).wait_recv()
                        onward(h, q, c, 0, False)
                        fwd(h, q, c).start()

                    @pl.when(pos + s <= per - 1)
                    def _():
                        h = v * per + pos + s
                        link_in(h, q, c).wait_recv()
                        onward(h, q, c, 1, False)
                        fwd(h, q, c).start()
            return carry

        if experts == 1:
            one(0, 0)
        else:
            lax.fori_loop(0, experts, one, 0)

    def project(t):
        h = index_of(t)
        for ci in range(n_pair):
            fwd_in(h, 0, pair_at(ci)).wait_recv()
        p1 = jnp.dot(xs[at_chunk(h), :], wab[...], preferred_element_type=F32)
        psx[h] = p1
        asx[0, h] = p1.astype(BF)
        ar(0, h, 0).start()
        for ci in range(n_pair):
            fwd_in(h, 1, pair_at(ci)).wait_recv()
        p2 = jnp.dot(ys[at_chunk(h), :], wc[...], preferred_element_type=F32)
        psy[h] = p2
        asy[0, h] = p2.astype(BF)
        ar(0, h, 1).start()

    def reduce_step(t, b):
        h = index_of(t)
        for part, (ps, send, recv) in enumerate(((psx, asx, arx), (psy, asy, ary))):
            ar(b, h, part).wait_recv()
            s = ps[h] + recv[b, h].astype(F32)
            ps[h] = s
            send[b + 1, h] = s.astype(BF)
            ar(b + 1, h, part).start()

    def finish(t):
        h = index_of(t)
        ar(nb - 1, h, 0).wait_recv()
        s = psx[h] + arx[nb - 1, h].astype(F32)
        gate_pre, up_pre = s[:, :hid], s[:, hid:]
        sig = 1.0 / (1.0 + jnp.exp(-gate_pre))
        sw = gate_pre * sig
        hidden = (sw * up_pre).astype(BF)
        hiddens[at_chunk(h), :] = hidden
        slope = up_pre * sig * (1.0 + gate_pre * (1.0 - sig))
        ar(nb - 1, h, 1).wait_recv()
        proj = psy[h] + ary[nb - 1, h].astype(F32)
        route = jnp.sum(hidden.astype(F32) * proj, axis=1, keepdims=True)
        d1 = (proj * slope).astype(BF)
        d2 = (proj * sw).astype(BF)
        deltas[at_chunk(h), 0:hid] = d1
        deltas[at_chunk(h), hid:] = d2
        part = lax.dot_general(
            jnp.concatenate([d1, d2], axis=1), wab[...], (((1,), (1,)), ((), ())),
            preferred_element_type=F32)
        rp[h, :, :, 0:lw] = part.reshape(2, half, lw).astype(BF)
        rp[h, :, :, lw:] = jnp.broadcast_to(route, (chunk, LANES)).reshape(2, half, LANES).astype(BF)
        r1(h).start()

    def r2(h, j):
        gp = flip(j)
        return rc(r2send.at[h, gp], ret.at[hi, g], r2s.at[h, j], r2r.at[hi, g], dp=gp, ep=h * 2 + lo)

    def r2_in(h, src):
        r = ret.at[h, src]
        return rc(r, r, r2r.at[h, src], r2r.at[h, src], ep=other)

    def send_back(t):
        h = index_of(t)
        r1(h).wait_recv()
        both = rp[h, lo].astype(F32) + r1recv[h].astype(F32)
        r2send[h] = both.reshape(n_dp, CAP, lw + LANES).astype(BF)
        for j in range(1, n_dp):
            r2(h, j).start()

        @pl.when(h != hi)
        def _():
            r2(h, 0).start()

        @pl.when(h == hi)
        def _():
            ret[hi, g] = r2send[h, g]

    early = n_hi - 2

    def flow(t, carry):
        s = t // experts

        @pl.when((s >= 1) & (s < per) & (t % experts == 0))
        def _():
            gather_step(s)

        for b in range(nb - 1):
            @pl.when((t >= 2 + b) & (t < n_hi + 2 + b))
            def _(b=b):
                reduce_step(t - 2 - b, b)

        @pl.when((t >= nb + 1) & (t < n_hi + nb + 1))
        def _():
            finish(t - nb - 1)

        @pl.when((t >= 1) & (t <= n_hi))
        def _():
            project(t - 1)

        @pl.when((t >= nb + 3) & (t < early + nb + 3))
        def _():
            send_back(t - nb - 3)
        return carry

    lax.fori_loop(1, n_hi + nb + 1, flow, 0)

    tile = 256 if lw % 256 == 0 else 128

    def wgrad(i, carry):
        ds = pl.ds(pl.multiple_of(i * tile, LANES), tile)
        dn = (((0,), (0,)), ((), ()))
        both = lax.dot_general(xs[:, ds], deltas[...], dn, preferred_element_type=F32).astype(BF)
        ga[ds, :] = both[:, :hid]
        gb[ds, :] = both[:, hid:]
        gc[ds, :] = lax.dot_general(ys[:, ds], hiddens[...], dn, preferred_element_type=F32).astype(BF)
        return carry

    lax.fori_loop(0, lw // tile, wgrad, 0)

    def rest(t, carry):
        send_back(t)
        return carry

    lax.fori_loop(early, n_hi, rest, 0)

    def collect(i, carry):
        h = lax.rem(hi + i, n_hi)
        for j in range(1, n_dp):
            r2_in(h, flip(j)).wait_recv()

        @pl.when(i >= 1)
        def _():
            r2_in(h, g).wait_recv()
        return carry

    lax.fori_loop(0, n_hi, collect, 0)

    for q in range(2):
        for j in range(n_dp):
            for i in range(experts):
                if i or j:
                    to_shard(j, i, q, flip(j)).wait_send()

    def drain(i, carry):
        h = lax.rem(hi + i, n_hi)
        p = h % per
        for q in range(2):
            for ci in range(n_pair):
                c = pair_at(ci)
                fwd(h, q, c).wait_send()

                @pl.when(p <= pos)
                def _():
                    onward(h, q, c, 0, True)

                @pl.when(p >= pos)
                def _():
                    onward(h, q, c, 1, True)
        for b in range(nb):
            for part in range(2):
                ar(b, h, part).wait_send()
        r1(h).wait_send()
        for j in range(1, n_dp):
            r2(h, j).wait_send()

        @pl.when(i >= 1)
        def _():
            r2(h, 0).wait_send()
        return carry

    lax.fori_loop(0, n_hi, drain, 0)


def finish_kernel(
    ret, sel_ref, ga, gb, gc, ids_ref, rw_ref, ig_hbm, rg_ref, ga_out, gb_out, gc_out,
    obuf, sem_out, osem,
):
    n_hi, n_dp, _, wide = ret.shape
    per = SLICES // 2
    experts = n_hi // per
    places = experts * CAP
    lw = wide - LANES
    rows = sel_ref.shape[0]
    stride = ROUTED // experts
    outs = [
        pltpu.make_async_copy(src, dst, sem_out.at[i])
        for i, (src, dst) in enumerate(((ga, ga_out), (gb, gb_out), (gc, gc_out)))
    ]
    for c in outs:
        c.start()
    sel = sel_ref[...]
    selP = sel[:, :places].astype(BF)

    def total(j):
        parts = []
        for w in range(experts):
            acc = ret[w * per, j].astype(F32)
            for i in range(1, per):
                acc = acc + ret[w * per + i, j].astype(F32)
            parts.append(acc)
        return jnp.concatenate(parts, axis=0) if experts > 1 else parts[0]

    ocopies = []
    for j in range(n_dp):
        vals = total(j)
        if j == 0:
            route = vals[:, lw:]
        obuf[:, j * lw:(j + 1) * lw] = jnp.dot(
            selP, vals[:, :lw].astype(BF), preferred_element_type=F32).astype(BF)
        ds = pl.ds(j * lw, lw)
        c = pltpu.make_async_copy(obuf.at[:, ds], ig_hbm.at[:, ds], osem.at[j])
        c.start()
        ocopies.append(c)
    route = jnp.concatenate([route, jnp.zeros((LANES - places, LANES), F32)], axis=0).T[0:1]
    terms = sel * route
    pad = jnp.zeros((LANES - TOPK, rows), F32)
    ids = jnp.concatenate([ids_ref[...].astype(F32), pad], axis=0).T
    lane = lax.broadcasted_iota(jnp.int32, (rows, LANES), 1)
    wanted = jnp.where(lane < places, (lane // CAP) * stride, -1).astype(F32)
    rg = jnp.zeros((rows, LANES), F32)
    for k in range(TOPK):
        v = jnp.sum(jnp.where(ids[:, k:k + 1] == wanted, terms, 0.0), axis=1, keepdims=True)
        rg = jnp.where(lane == k, v, rg)
    rg_ref[...] = rg.T[:TOPK] / rw_ref[...].astype(F32)
    for c in outs + ocopies:
        c.wait()


def body(tokens, out_grad, expert_ids, route_weights, gate_matrix, up_matrix, down_matrix):
    n_dp, n_ep = lax.axis_size("dp"), lax.axis_size("ep")
    experts = n_ep // SLICES
    n_hi = n_ep // 2
    n_pair = n_dp // 2
    rows, width = tokens.shape
    lw, hid = gate_matrix.shape
    nb = n_dp.bit_length() - 1
    chunk = 2 * n_dp * CAP
    half = n_dp * CAP
    total = n_hi * chunk
    R = lw + LANES
    K = 2 * n_pair
    V = pltpu.VMEM
    D = lambda *s: pltpu.SemaphoreType.DMA(s)
    anyspec = pl.BlockSpec(memory_space=pl.ANY)
    vspec = pl.BlockSpec(memory_space=pltpu.VMEM)
    ids, rw = expert_ids.T, route_weights.T
    grad = jax.ShapeDtypeStruct((lw, hid), BF)
    ret, sel, ga, gb, gc = pl.pallas_call(
        functools.partial(kernel, n_dp, n_ep),
        out_shape=(
            V((n_hi, n_dp, CAP, R), BF), V((rows, LANES), F32),
            V((lw, hid), BF), V((lw, hid), BF), V((lw, hid), BF),
        ),
        in_specs=[anyspec] * 7,
        out_specs=(vspec,) * 5,
        scratch_shapes=[
            V((TOPK, rows), jnp.int32), V((TOPK, rows), BF),
            V((n_dp, rows, lw), BF), V((n_dp, rows, lw), BF), V((lw, 2 * hid), BF), V((lw, hid), BF),
            V((n_dp, experts, CAP, 2 * lw), BF), V((experts, n_dp, CAP, 2 * lw), BF),
            V((total, lw), BF), V((total, lw), BF),
            V((n_hi, chunk, 2 * hid), F32), V((n_hi, chunk, hid), F32),
            V((nb, n_hi, chunk, 2 * hid), BF), V((nb, n_hi, chunk, 2 * hid), BF),
            V((nb, n_hi, chunk, hid), BF), V((nb, n_hi, chunk, hid), BF),
            V((total, 2 * hid), BF), V((total, hid), BF),
            V((n_hi, 2, half, R), BF), V((n_hi, half, R), BF), V((n_hi, n_dp, CAP, R), BF),
            D(2, n_dp), D(2), D(3), D(2, n_dp, experts), D(2, experts, n_dp),
            D(n_hi, K), D(n_hi, K), D(n_hi, K), D(n_hi, K), D(n_hi, K),
            D(nb, n_hi, 2), D(nb, n_hi, 2), D(n_hi), D(n_hi), D(n_hi, n_dp), D(n_hi, n_dp),
        ],
        compiler_params=pltpu.CompilerParams(
            collective_id=0, has_side_effects=True, vmem_limit_bytes=VMEM_BYTES),
    )(tokens, out_grad, ids, rw, gate_matrix, up_matrix, down_matrix)
    keep = [pltpu.with_memory_space_constraint(a, pltpu.VMEM) for a in (ret, sel, ga, gb, gc)]
    ig, rg, ga, gb, gc = pl.pallas_call(
        finish_kernel,
        out_shape=(
            jax.ShapeDtypeStruct((rows, width), BF),
            jax.ShapeDtypeStruct((TOPK, rows), F32),
            grad, grad, grad,
        ),
        in_specs=[vspec] * 7,
        out_specs=(anyspec, vspec, anyspec, anyspec, anyspec),
        scratch_shapes=[V((rows, width), BF), D(3), D(n_dp)],
        compiler_params=pltpu.CompilerParams(vmem_limit_bytes=16 * 1024 * 1024),
    )(*keep, ids, rw)
    return ig, rg.T, ga, gb, gc


def solution(mesh):
    return jax.shard_map(
        body,
        mesh=mesh,
        in_specs=(
            P(("dp", "ep"), None),
            P(("dp", "ep"), None),
            P(("dp", "ep"), None),
            P(("dp", "ep"), None),
            P("dp", "ep"),
            P("dp", "ep"),
            P("dp", "ep"),
        ),
        out_specs=(
            P(("dp", "ep"), None),
            P(("dp", "ep"), None),
            P("dp", "ep"),
            P("dp", "ep"),
            P("dp", "ep"),
        ),
        check_vma=False,
    )
```

time: 62.8 us -> 54 us (0.86)
  Pallas kernels: 61.9 us -> 53.1 us
    pallas_call x1, Pallas kernels: 56.9 us -> 50.4 us  [body(): pl.pallas_call(functools.partial(kernel, n_dp, n_ep), out_shape=(V((n_hi,...]
    pallas_call x1, Pallas kernels: 5.06 us -> 2.78 us  [body(): pl.pallas_call(finish_kernel, out_shape=(jax.ShapeDtypeStruct((rows, widt...]
where the time goes in v1:
time: 54 us; the launch traced here: 53.8 us
  Pallas kernels  53.1 us (98%)
  between operations  0.67 us (1%)
    pallas_call x1, Pallas kernels, body(): pl.pallas_call(functools.partial(kernel, n_dp, n_ep), out_shape=(V((n_hi,...  50.4 us
    pallas_call x1, Pallas kernels, body(): pl.pallas_call(finish_kernel, out_shape=(jax.ShapeDtypeStruct((rows, widt...  2.78 us

profile of v1, /device:TPU:0, one launch (start us, length us, event | category | flops | bytes accessed | tf_op | source)
XLA Modules:
  0.0 53.8 jit_solution(16163312501111052364)
XLA Ops:
  0.6 0.0 copy-start
  0.6 0.0 copy-start.1
  0.7 50.4 %shard_map.110 = (bf16[4,4,8,1920]{3,2,1,0:T(8,128)(2,1)S(1)}, f32[128,128]{1,0:T(8,128)S(1)}, bf16[1792,256]{1,0:T(8,128)(2,1)S(1)}, bf16[1792,256]{1,0:T(8,128)(2,1)S(1)}, bf16[1792,256]{1,0:T(8,128)(2,1)S(1)}) custom-call(bf16[128,7168]{1,0:T(8,128)(2,1)} %tok_hbm.1, bf16[128,7168]{1,0:T(8,128)(2,1)} %grad_hbm.1, s32[8,128]{1,0:T(8,128)} %bitcast.3, ...), custom_call_target="tpu_custom_call" | custom-call | tf_op jit(solution)/shard_map/pallas_call | solution.py:504
  51.0 0.0 copy-done
  51.0 0.0 copy-done.1
  51.0 2.8 %shard_map.111 = (bf16[128,7168]{1,0:T(8,128)(2,1)}, f32[8,128]{1,0:T(8,128)}, bf16[1792,256]{1,0:T(8,128)(2,1)}, bf16[1792,256]{1,0:T(8,128)(2,1)}, bf16[1792,256]{1,0:T(8,128)(2,1)}) custom-call(bf16[4,4,8,1920]{3,2,1,0:T(8,128)(2,1)S(1)} %get-tuple-element.15.ret, f32[128,128]{1,0:T(8,128)S(1)} %get-tuple-element.16.sel_ref, ...), custom_call_target="tpu_custom_call" | custom-call | tf_op jit(solution)/shard_map/pallas_call | solution.py:530
Async XLA Ops:
  0.6 50.4 %copy-start = (s32[128,8]{0,1:T(8,128)S(1)}, s32[128,8]{0,1:T(8,128)}, u32[]{:S(2)}) copy-start(s32[128,8]{0,1:T(8,128)} %param.9) | copy-start | bytes 12292
  0.6 50.4 %copy-start.1 = (bf16[128,8]{0,1:T(8,128)(2,1)S(1)}, bf16[128,8]{0,1:T(8,128)(2,1)}, u32[]{:S(2)}) copy-start(bf16[128,8]{0,1:T(8,128)(2,1)} %param.10) | copy-start | bytes 6148

commit v2 on v1

--- a/solution.py
+++ b/solution.py
@@ -21,10 +21,10 @@
 def kernel(
     n_dp, n_ep,
     tok_hbm, grad_hbm, ids_hbm, rw_hbm, a_hbm, b_hbm, c_hbm,
-    ret, sel_ref, ga, gb, gc,
-    ids_buf, rw_buf, tokbuf, gradbuf, wab, wc, send1, shard, xs, ys,
-    psx, psy, asx, arx, asy, ary, deltas, hiddens, rp, r1recv, r2send,
-    in_sem, id_sem, w_sem, s1s, s1r, sus, sds, slr, sfs, sfr, ars, arr, r1s, r1r, r2s, r2r,
+    ret, rret, sel_ref, ga, gb, gc,
+    ids_buf, rw_buf, tokbuf, gradbuf, w3, send1, shard, xs, ys,
+    psx, psy, asx, arx, asy, ary, deltas, hiddens, rp, r1recv, r2send, rsend,
+    in_sem, id_sem, out_sem, s1r, slr, sfr, arr, r1r,
 ):
     experts = n_ep // SLICES
     stride = ROUTED // experts
@@ -37,6 +37,8 @@
     nb = n_dp.bit_length() - 1
     chunk = 2 * n_dp * CAP
     half = n_dp * CAP
+    wab, wc = w3.at[:, pl.ds(0, 2 * hid)], w3.at[:, pl.ds(2 * hid, hid)]
+    w_sem, s1s, sus, sds, sfs, asxs, asys, r1s, r2s, r2r, rts, rtr = (out_sem.at[i] for i in range(12))
     g = lax.axis_index("dp")
     e = lax.axis_index("ep")
     hi, lo = e // 2, e % 2
@@ -75,12 +77,12 @@
             gp = flip(j)
             ds = pl.ds(pl.multiple_of(gp * lw, LANES), lw)
             c = pltpu.make_async_copy(src.at[:, ds], buf.at[j], in_sem.at[q, j])
-            c.start()
+            if q == 0:
+                c.start()
             loads.append((q, j, gp, buf, c))
     wloads = [
-        pltpu.make_async_copy(a_hbm, wab.at[:, pl.ds(0, hid)], w_sem.at[0]),
-        pltpu.make_async_copy(b_hbm, wab.at[:, pl.ds(hid, hid)], w_sem.at[1]),
-        pltpu.make_async_copy(c_hbm, wc, w_sem.at[2]),
+        pltpu.make_async_copy(w, w3.at[:, pl.ds(i * hid, hid)], w_sem)
+        for i, w in enumerate((a_hbm, b_hbm, c_hbm))
     ]
 
     barrier = pltpu.get_barrier_semaphore()
@@ -104,6 +106,9 @@
 
     for c in id_copies:
         c.wait()
+    for q, j, gp, buf, c in loads:
+        if q:
+            c.start()
     pad = jnp.zeros((LANES - TOPK, rows), F32)
     ids = jnp.concatenate([ids_buf[...].astype(F32), pad], axis=0).T
     rw = jnp.concatenate([rw_buf[...].astype(F32), pad], axis=0).T
@@ -128,7 +133,7 @@
     def to_shard(j, i, q, gp):
         v = line(i)
         return rc(send1.at[j, v, :, pieces[q]], shard.at[mine_w, g, :, pieces[q]],
-                  s1s.at[q, j, i], s1r.at[q, mine_w, g], dp=gp, ep=place(v))
+                  s1s, s1r.at[q, mine_w, g], dp=gp, ep=place(v))
 
     def shard_in(q, v, src):
         r = shard.at[v, src, :, pieces[q]]
@@ -173,7 +178,7 @@
         k = q * n_pair + c
         r = piece(q, h, lo, c)
         to = e + 2 - 4 * up
-        return rc(r, r, (sds if up else sus).at[h, k], slr.at[h, k], ep=to)
+        return rc(r, r, sds if up else sus, slr.at[h, k], ep=to)
 
     def link_in(h, q, c):
         k = q * n_pair + c
@@ -183,18 +188,24 @@
     def fwd(h, q, c):
         k = q * n_pair + c
         r = piece(q, h, lo, c)
-        return rc(r, r, sfs.at[h, k], sfr.at[h, k], ep=other)
+        return rc(r, r, sfs, sfr.at[h, k], ep=other)
+
+    def cross(h, q, c, up):
+        k = q * n_pair + c
+        r = piece(q, h, 1 - lo, c)
+        return rc(r, r, sds if up else sus, sfr.at[h, k], ep=e + 2 - 4 * up)
 
     def fwd_in(h, q, c):
         k = q * n_pair + c
         r = piece(q, h, 1 - lo, c)
         return rc(r, r, sfr.at[h, k], sfr.at[h, k], ep=other)
 
-    def onward(h, q, c, up, wait):
+    def onward(h, q, c, up):
         @pl.when((pos > 0) if up else (pos < per - 1))
         def _():
-            d = link(h, q, c, up)
-            d.wait_send() if wait else d.start()
+            link(h, q, c, up).start()
+
+    inner = (pos > 0) & (pos < per - 1)
 
     for ci in range(n_pair):
         c = pair_at(ci)
@@ -208,74 +219,99 @@
                         shard_in(q, v, src).wait_recv()
                 both = shard[v, pl.ds(2 * c, 2), :, q * lw:(q + 1) * lw]
                 (ys if q else xs)[rows_at(h, lo, c), :] = both.astype(F32).reshape(PAIR, lw).astype(BF)
-                onward(h, q, c, 0, False)
-                onward(h, q, c, 1, False)
+                onward(h, q, c, 0)
+                onward(h, q, c, 1)
                 fwd(h, q, c).start()
-    for c in wloads:
-        c.wait()
+    pltpu.make_async_copy(w3, w3, w_sem).wait()
 
     def ar(b, h, part):
         bit = 1 << b
         peer = g + (1 - 2 * ((g // bit) % 2)) * bit
         src, dst = ((asx, arx), (asy, ary))[part]
-        return rc(src.at[b, h], dst.at[b, h], ars.at[b, h, part], arr.at[b, h, part], dp=peer)
+        return rc(src.at[b, h], dst.at[b, h], (asxs, asys)[part], arr.at[b, h, part], dp=peer)
 
     def at_chunk(h):
         return pl.ds(pl.multiple_of(h * chunk, PAIR), chunk)
 
     def r1(h):
-        return rc(rp.at[h, 1 - lo], r1recv.at[h], r1s.at[h], r1r.at[h], ep=other)
-
-    def chunk_of(t):
-        return at_order(t // experts), t % experts
-
-    def index_of(t):
-        p, v = chunk_of(t)
-        return v * per + p
-
-    def gather_step(s):
-        def one(v, carry):
-            for q in range(2):
+        return rc(rp.at[h, 1 - lo], r1recv.at[h], r1s, r1r.at[h], ep=other)
+
+    def over(stage):
+        if experts == 1:
+            stage(0)
+        else:
+            lax.fori_loop(0, experts, lambda v, carry: (stage(v), carry)[1], 0)
+
+    def gather_step(s, v):
+        for q in range(2):
+            for ci in range(n_pair):
+                c = pair_at(ci)
+                if s == 1:
+                    @pl.when(jnp.logical_not(inner))
+                    def _():
+                        h = v * per + pos
+                        fwd_in(h, q, c).wait_recv()
+                        for up in range(2):
+                            @pl.when((pos > 0) if up else (pos == 0))
+                            def _():
+                                cross(h, q, c, up).start()
+
+                for up in range(2):
+                    p = pos + s if up else pos - s
+
+                    @pl.when((p <= per - 1) if up else (p >= 0))
+                    def _():
+                        h = v * per + p
+                        link_in(h, q, c).wait_recv()
+                        onward(h, q, c, up)
+                        if s == 1:
+                            @pl.when(jnp.logical_not(inner & ((p == 0) | (p == per - 1))))
+                            def _():
+                                fwd(h, q, c).start()
+                        elif s == 2 or q == 0:
+                            fwd(h, q, c).start()
+
+    def cross_far(v):
+        for ci in range(n_pair):
+            c = pair_at(ci)
+
+            @pl.when(inner)
+            def _():
+                h = v * per + at_order(per - 1)
+                fwd_in(h, 1, c).wait_recv()
+                for up in range(2):
+                    @pl.when((pos < per // 2) if up else (pos >= per // 2))
+                    def _():
+                        cross(h, 1, c, up).start()
+
+    def project(k, v):
+        h = v * per + at_order(k)
+
+        def arrived(q):
+            def wait():
                 for ci in range(n_pair):
-                    c = pair_at(ci)
-
-                    @pl.when(pos >= s)
-                    def _():
-                        h = v * per + pos - s
-                        link_in(h, q, c).wait_recv()
-                        onward(h, q, c, 0, False)
-                        fwd(h, q, c).start()
-
-                    @pl.when(pos + s <= per - 1)
-                    def _():
-                        h = v * per + pos + s
-                        link_in(h, q, c).wait_recv()
-                        onward(h, q, c, 1, False)
-                        fwd(h, q, c).start()
-            return carry
-
-        if experts == 1:
-            one(0, 0)
-        else:
-            lax.fori_loop(0, experts, one, 0)
-
-    def project(t):
-        h = index_of(t)
-        for ci in range(n_pair):
-            fwd_in(h, 0, pair_at(ci)).wait_recv()
+                    fwd_in(h, q, pair_at(ci)).wait_recv()
+
+            if k == 0:
+                pl.when(inner)(wait)
+            elif k == per - 1 and q:
+                pl.when(jnp.logical_not(inner))(wait)
+            else:
+                wait()
+
+        arrived(0)
         p1 = jnp.dot(xs[at_chunk(h), :], wab[...], preferred_element_type=F32)
         psx[h] = p1
         asx[0, h] = p1.astype(BF)
         ar(0, h, 0).start()
-        for ci in range(n_pair):
-            fwd_in(h, 1, pair_at(ci)).wait_recv()
+        arrived(1)
         p2 = jnp.dot(ys[at_chunk(h), :], wc[...], preferred_element_type=F32)
         psy[h] = p2
         asy[0, h] = p2.astype(BF)
         ar(0, h, 1).start()
 
-    def reduce_step(t, b):
-        h = index_of(t)
+    def reduce_step(k, b, v):
+        h = v * per + at_order(k)
         for part, (ps, send, recv) in enumerate(((psx, asx, arx), (psy, asy, ary))):
             ar(b, h, part).wait_recv()
             s = ps[h] + recv[b, h].astype(F32)
@@ -283,8 +319,8 @@
             send[b + 1, h] = s.astype(BF)
             ar(b + 1, h, part).start()
 
-    def finish(t):
-        h = index_of(t)
+    def finish(k, v):
+        h = v * per + at_order(k)
         ar(nb - 1, h, 0).wait_recv()
         s = psx[h] + arx[nb - 1, h].astype(F32)
         gate_pre, up_pre = s[:, :hid], s[:, hid:]
@@ -303,23 +339,26 @@
         part = lax.dot_general(
             jnp.concatenate([d1, d2], axis=1), wab[...], (((1,), (1,)), ((), ())),
             preferred_element_type=F32)
-        rp[h, :, :, 0:lw] = part.reshape(2, half, lw).astype(BF)
-        rp[h, :, :, lw:] = jnp.broadcast_to(route, (chunk, LANES)).reshape(2, half, LANES).astype(BF)
-        r1(h).start()
+        rp[h] = part.reshape(2, half, lw).astype(BF)
+        rsend[h] = jnp.broadcast_to(route, (chunk, LANES)).reshape(2, n_dp, CAP, LANES).astype(BF)
+        for l in range(2):
+            @pl.when(h * 2 + l != e)
+            def _():
+                rc(rsend.at[h, l, g], rret.at[e], rts, rtr, ep=h * 2 + l).start()
+
+            @pl.when(h * 2 + l == e)
+            def _():
+                rret[e] = rsend[h, l, g]
 
     def r2(h, j):
         gp = flip(j)
-        return rc(r2send.at[h, gp], ret.at[hi, g], r2s.at[h, j], r2r.at[hi, g], dp=gp, ep=h * 2 + lo)
-
-    def r2_in(h, src):
-        r = ret.at[h, src]
-        return rc(r, r, r2r.at[h, src], r2r.at[h, src], ep=other)
-
-    def send_back(t):
-        h = index_of(t)
+        return rc(r2send.at[h, gp], ret.at[hi * n_dp + g], r2s, r2r, dp=gp, ep=h * 2 + lo)
+
+    def send_back(k, v):
+        h = v * per + at_order(k)
         r1(h).wait_recv()
         both = rp[h, lo].astype(F32) + r1recv[h].astype(F32)
-        r2send[h] = both.reshape(n_dp, CAP, lw + LANES).astype(BF)
+        r2send[h] = both.reshape(n_dp, CAP, lw).astype(BF)
         for j in range(1, n_dp):
             r2(h, j).start()
 
@@ -329,36 +368,51 @@
 
         @pl.when(h == hi)
         def _():
-            ret[hi, g] = r2send[h, g]
-
-    early = n_hi - 2
-
-    def flow(t, carry):
-        s = t // experts
-
-        @pl.when((s >= 1) & (s < per) & (t % experts == 0))
-        def _():
-            gather_step(s)
-
+            ret[hi * n_dp + g] = r2send[h, g]
+
+    def G(s):
+        over(functools.partial(gather_step, s))
+
+    def P(k):
+        over(functools.partial(project, k))
+
+    def A(k):
         for b in range(nb - 1):
-            @pl.when((t >= 2 + b) & (t < n_hi + 2 + b))
-            def _(b=b):
-                reduce_step(t - 2 - b, b)
-
-        @pl.when((t >= nb + 1) & (t < n_hi + nb + 1))
-        def _():
-            finish(t - nb - 1)
-
-        @pl.when((t >= 1) & (t <= n_hi))
-        def _():
-            project(t - 1)
-
-        @pl.when((t >= nb + 3) & (t < early + nb + 3))
-        def _():
-            send_back(t - nb - 3)
-        return carry
-
-    lax.fori_loop(1, n_hi + nb + 1, flow, 0)
+            over(functools.partial(reduce_step, k, b))
+
+    def F(k):
+        over(functools.partial(finish, k))
+
+    def S(k):
+        over(lambda v: r1(v * per + at_order(k)).start())
+
+    def R(k):
+        over(functools.partial(send_back, k))
+
+    G(1)
+    P(0)
+    A(0)
+    G(2)
+    P(1)
+    A(1)
+    F(0)
+    G(3)
+    P(2)
+    over(cross_far)
+    A(2)
+    F(1)
+    S(1)
+    S(0)
+    P(3)
+    A(3)
+    F(2)
+    S(2)
+    R(1)
+    F(3)
+    S(3)
+    R(0)
+    R(2)
+    R(3)
 
     tile = 256 if lw % 256 == 0 else 128
 
@@ -373,69 +427,45 @@
 
     lax.fori_loop(0, lw // tile, wgrad, 0)
 
-    def rest(t, carry):
-        send_back(t)
-        return carry
-
-    lax.fori_loop(early, n_hi, rest, 0)
-
-    def collect(i, carry):
-        h = lax.rem(hi + i, n_hi)
-        for j in range(1, n_dp):
-            r2_in(h, flip(j)).wait_recv()
-
-        @pl.when(i >= 1)
-        def _():
-            r2_in(h, g).wait_recv()
-        return carry
-
-    lax.fori_loop(0, n_hi, collect, 0)
-
-    for q in range(2):
-        for j in range(n_dp):
-            for i in range(experts):
-                if i or j:
-                    to_shard(j, i, q, flip(j)).wait_send()
-
-    def drain(i, carry):
-        h = lax.rem(hi + i, n_hi)
-        p = h % per
-        for q in range(2):
-            for ci in range(n_pair):
-                c = pair_at(ci)
-                fwd(h, q, c).wait_send()
-
-                @pl.when(p <= pos)
-                def _():
-                    onward(h, q, c, 0, True)
-
-                @pl.when(p >= pos)
-                def _():
-                    onward(h, q, c, 1, True)
-        for b in range(nb):
-            for part in range(2):
-                ar(b, h, part).wait_send()
-        r1(h).wait_send()
-        for j in range(1, n_dp):
-            r2(h, j).wait_send()
-
-        @pl.when(i >= 1)
-        def _():
-            r2(h, 0).wait_send()
-        return carry
-
-    lax.fori_loop(0, n_hi, drain, 0)
+    def settle(ref, sem):
+        pltpu.make_async_copy(ref, ref, sem).wait()
+
+    back, routes = ret.at[pl.ds(0, n_hi * n_dp - 1)], rret.at[pl.ds(0, n_ep - 1)]
+    settle(back, r2r)
+    settle(routes, rtr)
+    settle(back, r2s)
+    settle(routes, rts)
+    settle(r1recv, r1s)
+    settle(asx, asxs)
+    settle(asy, asys)
+    settle(xs.at[pl.ds(0, PAIR * (n_dp * experts - 1)), :], s1s)
+    K = 2 * n_pair
+    for at in range(per):
+        ends = at in (0, per - 1)
+        crossing = {0: K, per - 2: n_pair}
+        down = per - 1 - at
+        sent = (
+            (sus, (at + 1) * K + crossing.get(at, 0) if down else 0),
+            (sds, (down + 1) * K + crossing.get(down, 0) if at else 0),
+            (sfs, (per - 1) * K + (n_pair if ends else 0)),
+        )
+
+        @pl.when(pos == at)
+        def _(sent=sent):
+            for sem, count in sent:
+                if count:
+                    settle(xs.at[pl.ds(0, PAIR * count * experts), :], sem)
 
 
 def finish_kernel(
-    ret, sel_ref, ga, gb, gc, ids_ref, rw_ref, ig_hbm, rg_ref, ga_out, gb_out, gc_out,
+    ret, rret, sel_ref, ga, gb, gc, ids_ref, rw_ref, ig_hbm, rg_ref, ga_out, gb_out, gc_out,
     obuf, sem_out, osem,
 ):
-    n_hi, n_dp, _, wide = ret.shape
     per = SLICES // 2
-    experts = n_hi // per
+    experts = rret.shape[0] // SLICES
+    n_dp = ret.shape[0] // (experts * per)
     places = experts * CAP
-    lw = wide - LANES
+    lw = ret.shape[2]
     rows = sel_ref.shape[0]
     stride = ROUTED // experts
     outs = [
@@ -447,26 +477,24 @@
     sel = sel_ref[...]
     selP = sel[:, :places].astype(BF)
 
-    def total(j):
+    def total(ref, base, step, count):
         parts = []
         for w in range(experts):
-            acc = ret[w * per, j].astype(F32)
-            for i in range(1, per):
-                acc = acc + ret[w * per + i, j].astype(F32)
+            acc = ref[w * count * step + base].astype(F32)
+            for i in range(1, count):
+                acc = acc + ref[(w * count + i) * step + base].astype(F32)
             parts.append(acc)
         return jnp.concatenate(parts, axis=0) if experts > 1 else parts[0]
 
     ocopies = []
     for j in range(n_dp):
-        vals = total(j)
-        if j == 0:
-            route = vals[:, lw:]
         obuf[:, j * lw:(j + 1) * lw] = jnp.dot(
-            selP, vals[:, :lw].astype(BF), preferred_element_type=F32).astype(BF)
+            selP, total(ret, j, n_dp, per).astype(BF), preferred_element_type=F32).astype(BF)
         ds = pl.ds(j * lw, lw)
         c = pltpu.make_async_copy(obuf.at[:, ds], ig_hbm.at[:, ds], osem.at[j])
         c.start()
         ocopies.append(c)
+    route = total(rret, 0, 1, SLICES)
     route = jnp.concatenate([route, jnp.zeros((LANES - places, LANES), F32)], axis=0).T[0:1]
     terms = sel * route
     pad = jnp.zeros((LANES - TOPK, rows), F32)
@@ -493,7 +521,6 @@
     chunk = 2 * n_dp * CAP
     half = n_dp * CAP
     total = n_hi * chunk
-    R = lw + LANES
     K = 2 * n_pair
     V = pltpu.VMEM
     D = lambda *s: pltpu.SemaphoreType.DMA(s)
@@ -501,32 +528,31 @@
     vspec = pl.BlockSpec(memory_space=pltpu.VMEM)
     ids, rw = expert_ids.T, route_weights.T
     grad = jax.ShapeDtypeStruct((lw, hid), BF)
-    ret, sel, ga, gb, gc = pl.pallas_call(
+    kept = pl.pallas_call(
         functools.partial(kernel, n_dp, n_ep),
         out_shape=(
-            V((n_hi, n_dp, CAP, R), BF), V((rows, LANES), F32),
+            V((n_hi * n_dp, CAP, lw), BF), V((n_ep, CAP, LANES), BF), V((rows, LANES), F32),
             V((lw, hid), BF), V((lw, hid), BF), V((lw, hid), BF),
         ),
         in_specs=[anyspec] * 7,
-        out_specs=(vspec,) * 5,
+        out_specs=(vspec,) * 6,
         scratch_shapes=[
             V((TOPK, rows), jnp.int32), V((TOPK, rows), BF),
-            V((n_dp, rows, lw), BF), V((n_dp, rows, lw), BF), V((lw, 2 * hid), BF), V((lw, hid), BF),
+            V((n_dp, rows, lw), BF), V((n_dp, rows, lw), BF), V((lw, 3 * hid), BF),
             V((n_dp, experts, CAP, 2 * lw), BF), V((experts, n_dp, CAP, 2 * lw), BF),
             V((total, lw), BF), V((total, lw), BF),
             V((n_hi, chunk, 2 * hid), F32), V((n_hi, chunk, hid), F32),
             V((nb, n_hi, chunk, 2 * hid), BF), V((nb, n_hi, chunk, 2 * hid), BF),
             V((nb, n_hi, chunk, hid), BF), V((nb, n_hi, chunk, hid), BF),
             V((total, 2 * hid), BF), V((total, hid), BF),
-            V((n_hi, 2, half, R), BF), V((n_hi, half, R), BF), V((n_hi, n_dp, CAP, R), BF),
-            D(2, n_dp), D(2), D(3), D(2, n_dp, experts), D(2, experts, n_dp),
-            D(n_hi, K), D(n_hi, K), D(n_hi, K), D(n_hi, K), D(n_hi, K),
-            D(nb, n_hi, 2), D(nb, n_hi, 2), D(n_hi), D(n_hi), D(n_hi, n_dp), D(n_hi, n_dp),
+            V((n_hi, 2, half, lw), BF), V((n_hi, half, lw), BF), V((n_hi, n_dp, CAP, lw), BF),
+            V((n_hi, 2, n_dp, CAP, LANES), BF),
+            D(2, n_dp), D(2), D(12), D(2, experts, n_dp), D(n_hi, K), D(n_hi, K), D(nb, n_hi, 2), D(n_hi),
         ],
         compiler_params=pltpu.CompilerParams(
             collective_id=0, has_side_effects=True, vmem_limit_bytes=VMEM_BYTES),
     )(tokens, out_grad, ids, rw, gate_matrix, up_matrix, down_matrix)
-    keep = [pltpu.with_memory_space_constraint(a, pltpu.VMEM) for a in (ret, sel, ga, gb, gc)]
+    kept = [pltpu.with_memory_space_constraint(a, pltpu.VMEM) for a in kept]
     ig, rg, ga, gb, gc = pl.pallas_call(
         finish_kernel,
         out_shape=(
@@ -534,11 +560,11 @@
             jax.ShapeDtypeStruct((TOPK, rows), F32),
             grad, grad, grad,
         ),
-        in_specs=[vspec] * 7,
+        in_specs=[vspec] * 8,
         out_specs=(anyspec, vspec, anyspec, anyspec, anyspec),
         scratch_shapes=[V((rows, width), BF), D(3), D(n_dp)],
         compiler_params=pltpu.CompilerParams(vmem_limit_bytes=16 * 1024 * 1024),
-    )(*keep, ids, rw)
+    )(*kept, ids, rw)
     return ig, rg.T, ga, gb, gc
 
 

time: 54 us -> 49.9 us (0.924)
  Pallas kernels: 53.1 us -> 49 us
    pallas_call x1, Pallas kernels: 50.4 us -> 46.3 us  [body(): pl.pallas_call(functools.partial(kernel, n_dp, n_ep), out_shape=(V((n_hi...]
where the time goes in v2:
time: 49.9 us; the launch traced here: 49.7 us
  Pallas kernels  49 us (98%)
  between operations  0.67 us (1%)
    pallas_call x1, Pallas kernels, body(): pl.pallas_call(functools.partial(kernel, n_dp, n_ep), out_shape=(V((n_hi...  46.3 us
    pallas_call x1, Pallas kernels, body(): pl.pallas_call(finish_kernel, out_shape=(jax.ShapeDtypeStruct((rows, widt...  2.79 us

profile of v2, /device:TPU:0, one launch (start us, length us, event | category | flops | bytes accessed | tf_op | source)
XLA Modules:
  0.0 49.7 jit_solution(9090195734657695187)
XLA Ops:
  0.6 0.0 copy-start
  0.6 0.0 copy-start.1
  0.7 46.3 %shard_map.110 = (bf16[16,8,1792]{2,1,0:T(8,128)(2,1)S(1)}, bf16[8,8,128]{2,1,0:T(8,128)(2,1)S(1)}, f32[128,128]{1,0:T(8,128)S(1)}, bf16[1792,256]{1,0:T(8,128)(...) custom-call(bf16[128,7168]{1,0:T(8,128)(2,1)} %tok_hbm.1, bf16[128,7168]{1,0:T(8,128)(2,1)} %grad_hbm.1, ...), custom_call_target="tpu_custom_call" | custom-call | tf_op jit(solution)/shard_map/pallas_call | solution.py:531
  46.9 0.0 copy-done
  46.9 0.0 copy-done.1
  46.9 2.8 %shard_map.111 = (bf16[128,7168]{1,0:T(8,128)(2,1)}, f32[8,128]{1,0:T(8,128)}, bf16[1792,256]{1,0:T(8,128)(2,1)}, bf16[1792,256]{1,0:T(8,128)(2,1)}, bf16[1792,256]{1,0:T(8,128)(2,1)}) custom-call(bf16[16,8,1792]{2,1,0:T(8,128)(2,1)S(1)} %get-tuple-element.16.ret, bf16[8,8,128]{2,1,0:T(8,128)(2,1)S(1)} %get-tuple-element.17.rret, ...), custom_call_target="tpu_custom_call" | custom-call | tf_op jit(solution)/shard_map/pallas_call | solution.py:556
Async XLA Ops:
  0.6 46.3 %copy-start = (s32[128,8]{0,1:T(8,128)S(1)}, s32[128,8]{0,1:T(8,128)}, u32[]{:S(2)}) copy-start(s32[128,8]{0,1:T(8,128)} %param.9) | copy-start | bytes 12292
  0.6 46.3 %copy-start.1 = (bf16[128,8]{0,1:T(8,128)(2,1)S(1)}, bf16[128,8]{0,1:T(8,128)(2,1)}, u32[]{:S(2)}) copy-start(bf16[128,8]{0,1:T(8,128)(2,1)} %param.10) | copy-start | bytes 6148

commit v3 on v2

--- a/solution.py
+++ b/solution.py
@@ -109,24 +109,23 @@
     for q, j, gp, buf, c in loads:
         if q:
             c.start()
-    pad = jnp.zeros((LANES - TOPK, rows), F32)
-    ids = jnp.concatenate([ids_buf[...].astype(F32), pad], axis=0).T
-    rw = jnp.concatenate([rw_buf[...].astype(F32), pad], axis=0).T
-    lane = lax.broadcasted_iota(jnp.int32, (rows, LANES), 1)
-    wanted = jnp.where(lane < places, (lane // CAP) * stride, -1).astype(F32)
-    hits = jnp.zeros((rows, LANES), F32)
-    wts = jnp.zeros((rows, LANES), F32)
-    for k in range(TOPK):
-        m = ids[:, k:k + 1] == wanted
-        hits = hits + jnp.where(m, 1.0, 0.0)
-        wts = wts + jnp.where(m, rw[:, k:k + 1], 0.0)
+    ids, rw = ids_buf[...], rw_buf[...].astype(F32)
+    spread = lambda a: jnp.broadcast_to(jnp.sum(a, axis=0, keepdims=True), (CAP, rows))
+    hits, wts = [], []
+    for w in range(experts):
+        m = ids == w * stride
+        hits.append(spread(jnp.where(m, 1.0, 0.0)))
+        wts.append(spread(jnp.where(m, rw, 0.0)))
+    hits = jnp.concatenate(hits, axis=0) if experts > 1 else hits[0]
+    wts = jnp.concatenate(wts, axis=0) if experts > 1 else wts[0]
     tr = lax.broadcasted_iota(jnp.int32, (rows, rows), 0)
     tc = lax.broadcasted_iota(jnp.int32, (rows, rows), 1)
-    lower = jnp.where(tc < tr, 1.0, 0.0).astype(BF)
-    slot = jnp.dot(lower, hits.astype(BF), preferred_element_type=F32)
-    sel = jnp.where(slot == (lane % CAP).astype(F32), hits, 0.0)
+    before = jnp.where(tr < tc, 1.0, 0.0).astype(BF)
+    slot = jnp.dot(hits.astype(BF), before, preferred_element_type=F32)
+    place_in = lax.broadcasted_iota(jnp.int32, (places, rows), 0) % CAP
+    sel = jnp.where(slot == place_in.astype(F32), hits, 0.0)
     sel_ref[...] = sel
-    picks = (sel.T[:places].astype(BF), (sel * wts).T[:places].astype(BF))
+    picks = (sel.astype(BF), (sel * wts).astype(BF))
 
     pieces = (pl.ds(0, lw), pl.ds(lw, lw))
 
@@ -161,7 +160,8 @@
 
     def at_order(k):
         m = jnp.where(pos < per - 1 - pos, pos, per - 1 - pos)
-        near = jnp.where(k % 2 == 1, pos - (k + 1) // 2, pos + k // 2)
+        side = jnp.where(pos < per // 2, 1, -1)
+        near = pos + side * ((k + 1) // 2 if k % 2 else -(k // 2))
         far = jnp.where(pos < per - 1 - pos, k, per - 1 - k)
         return jnp.where(k <= 2 * m, near, far)
 
@@ -233,8 +233,11 @@
     def at_chunk(h):
         return pl.ds(pl.multiple_of(h * chunk, PAIR), chunk)
 
-    def r1(h):
-        return rc(rp.at[h, 1 - lo], r1recv.at[h], r1s, r1r.at[h], ep=other)
+    def pair_rows(c):
+        return pl.ds(pl.multiple_of(c * PAIR, PAIR), PAIR)
+
+    def r1(h, c):
+        return rc(rp.at[h, 1 - lo, pair_rows(c)], r1recv.at[h, pair_rows(c)], r1s, r1r.at[h, c], ep=other)
 
     def over(stage):
         if experts == 1:
@@ -350,25 +353,28 @@
             def _():
                 rret[e] = rsend[h, l, g]
 
-    def r2(h, j):
-        gp = flip(j)
-        return rc(r2send.at[h, gp], ret.at[hi * n_dp + g], r2s, r2r, dp=gp, ep=h * 2 + lo)
-
     def send_back(k, v):
         h = v * per + at_order(k)
-        r1(h).wait_recv()
-        both = rp[h, lo].astype(F32) + r1recv[h].astype(F32)
-        r2send[h] = both.reshape(n_dp, CAP, lw).astype(BF)
-        for j in range(1, n_dp):
-            r2(h, j).start()
-
-        @pl.when(h != hi)
-        def _():
-            r2(h, 0).start()
-
-        @pl.when(h == hi)
-        def _():
-            ret[hi * n_dp + g] = r2send[h, g]
+        for ci in reversed(range(n_pair)):
+            c = pair_at(ci)
+            r1(h, c).wait_recv()
+            both = rp[h, lo, pair_rows(c)].astype(F32) + r1recv[h, pair_rows(c)].astype(F32)
+            r2send[h, pl.ds(2 * c, 2)] = both.reshape(2, CAP, lw).astype(BF)
+            for b in range(2):
+                gp = 2 * c + b
+
+                def pass_on():
+                    rc(r2send.at[h, gp], ret.at[hi * n_dp + g], r2s, r2r, dp=gp, ep=h * 2 + lo).start()
+
+                def keep():
+                    ret[hi * n_dp + g] = r2send[h, gp]
+
+                if ci or (k and experts == 1):
+                    pass_on()
+                else:
+                    mine = (h == hi) & (gp == g)
+                    pl.when(jnp.logical_not(mine))(pass_on)
+                    pl.when(mine)(keep)
 
     def G(s):
         over(functools.partial(gather_step, s))
@@ -384,7 +390,11 @@
         over(functools.partial(finish, k))
 
     def S(k):
-        over(lambda v: r1(v * per + at_order(k)).start())
+        def start(v):
+            for ci in reversed(range(n_pair)):
+                r1(v * per + at_order(k), pair_at(ci)).start()
+
+        over(start)
 
     def R(k):
         over(functools.partial(send_back, k))
@@ -396,13 +406,13 @@
     P(1)
     A(1)
     F(0)
+    pl.when(inner)(functools.partial(S, 0))
     G(3)
     P(2)
     over(cross_far)
     A(2)
     F(1)
     S(1)
-    S(0)
     P(3)
     A(3)
     F(2)
@@ -410,9 +420,10 @@
     R(1)
     F(3)
     S(3)
-    R(0)
+    pl.when(jnp.logical_not(inner))(functools.partial(S, 0))
     R(2)
     R(3)
+    R(0)
 
     tile = 256 if lw % 256 == 0 else 128
 
@@ -464,9 +475,8 @@
     per = SLICES // 2
     experts = rret.shape[0] // SLICES
     n_dp = ret.shape[0] // (experts * per)
-    places = experts * CAP
     lw = ret.shape[2]
-    rows = sel_ref.shape[0]
+    rows = sel_ref.shape[1]
     stride = ROUTED // experts
     outs = [
         pltpu.make_async_copy(src, dst, sem_out.at[i])
@@ -475,7 +485,7 @@
     for c in outs:
         c.start()
     sel = sel_ref[...]
-    selP = sel[:, :places].astype(BF)
+    picks = sel.astype(BF)
 
     def total(ref, base, step, count):
         parts = []
@@ -488,24 +498,20 @@
 
     ocopies = []
     for j in range(n_dp):
-        obuf[:, j * lw:(j + 1) * lw] = jnp.dot(
-            selP, total(ret, j, n_dp, per).astype(BF), preferred_element_type=F32).astype(BF)
+        obuf[:, j * lw:(j + 1) * lw] = lax.dot_general(
+            picks, total(ret, j, n_dp, per).astype(BF), (((0,), (0,)), ((), ())),
+            preferred_element_type=F32).astype(BF)
         ds = pl.ds(j * lw, lw)
         c = pltpu.make_async_copy(obuf.at[:, ds], ig_hbm.at[:, ds], osem.at[j])
         c.start()
         ocopies.append(c)
-    route = total(rret, 0, 1, SLICES)
-    route = jnp.concatenate([route, jnp.zeros((LANES - places, LANES), F32)], axis=0).T[0:1]
-    terms = sel * route
-    pad = jnp.zeros((LANES - TOPK, rows), F32)
-    ids = jnp.concatenate([ids_ref[...].astype(F32), pad], axis=0).T
-    lane = lax.broadcasted_iota(jnp.int32, (rows, LANES), 1)
-    wanted = jnp.where(lane < places, (lane // CAP) * stride, -1).astype(F32)
-    rg = jnp.zeros((rows, LANES), F32)
-    for k in range(TOPK):
-        v = jnp.sum(jnp.where(ids[:, k:k + 1] == wanted, terms, 0.0), axis=1, keepdims=True)
-        rg = jnp.where(lane == k, v, rg)
-    rg_ref[...] = rg.T[:TOPK] / rw_ref[...].astype(F32)
+    terms = sel * total(rret, 0, 1, SLICES)
+    ids = ids_ref[...]
+    rg = jnp.zeros((TOPK, rows), F32)
+    for w in range(experts):
+        v = jnp.sum(terms[w * CAP:(w + 1) * CAP], axis=0, keepdims=True)
+        rg = rg + jnp.where(ids == w * stride, v, 0.0)
+    rg_ref[...] = rg / rw_ref[...].astype(F32)
     for c in outs + ocopies:
         c.wait()
 
@@ -531,7 +537,7 @@
     kept = pl.pallas_call(
         functools.partial(kernel, n_dp, n_ep),
         out_shape=(
-            V((n_hi * n_dp, CAP, lw), BF), V((n_ep, CAP, LANES), BF), V((rows, LANES), F32),
+            V((n_hi * n_dp, CAP, lw), BF), V((n_ep, CAP, LANES), BF), V((experts * CAP, rows), F32),
             V((lw, hid), BF), V((lw, hid), BF), V((lw, hid), BF),
         ),
         in_specs=[anyspec] * 7,
@@ -547,7 +553,7 @@
             V((total, 2 * hid), BF), V((total, hid), BF),
             V((n_hi, 2, half, lw), BF), V((n_hi, half, lw), BF), V((n_hi, n_dp, CAP, lw), BF),
             V((n_hi, 2, n_dp, CAP, LANES), BF),
-            D(2, n_dp), D(2), D(12), D(2, experts, n_dp), D(n_hi, K), D(n_hi, K), D(nb, n_hi, 2), D(n_hi),
+            D(2, n_dp), D(2), D(12), D(2, experts, n_dp), D(n_hi, K), D(n_hi, K), D(nb, n_hi, 2), D(n_hi, n_pair),
         ],
         compiler_params=pltpu.CompilerParams(
             collective_id=0, has_side_effects=True, vmem_limit_bytes=VMEM_BYTES),

time: 49.9 us -> 46.7 us (0.936)
  Pallas kernels: 49 us -> 45.8 us
    pallas_call x1, Pallas kernels: 46.3 us -> 43.1 us  [body(): pl.pallas_call(functools.partial(kernel, n_dp, n_ep), out_shape=(V((n_hi...]
where the time goes in v3:
time: 46.7 us; the launch traced here: 46.5 us
  Pallas kernels  45.8 us (98%)
  between operations  0.67 us (1%)
    pallas_call x1, Pallas kernels, body(): pl.pallas_call(functools.partial(kernel, n_dp, n_ep), out_shape=(V((n_hi...  43.1 us
    pallas_call x1, Pallas kernels, body(): pl.pallas_call(finish_kernel, out_shape=(jax.ShapeDtypeStruct((rows, widt...  2.79 us

profile of v3, /device:TPU:0, one launch (start us, length us, event | category | flops | bytes accessed | tf_op | source)
XLA Modules:
  0.0 46.5 jit_solution(5287298432719773584)
XLA Ops:
  0.6 0.0 copy-start
  0.6 0.0 copy-start.1
  0.7 43.1 %shard_map.110 = (bf16[16,8,1792]{2,1,0:T(8,128)(2,1)S(1)}, bf16[8,8,128]{2,1,0:T(8,128)(2,1)S(1)}, f32[8,128]{1,0:T(8,128)S(1)}, bf16[1792,256]{1,0:T(8,128)(2,...) custom-call(bf16[128,7168]{1,0:T(8,128)(2,1)} %tok_hbm.1, bf16[128,7168]{1,0:T(8,128)(2,1)} %grad_hbm.1, ...), custom_call_target="tpu_custom_call" | custom-call | tf_op jit(solution)/shard_map/pallas_call | solution.py:537
  43.7 0.0 copy-done
  43.7 0.0 copy-done.1
  43.7 2.8 %shard_map.111 = (bf16[128,7168]{1,0:T(8,128)(2,1)}, f32[8,128]{1,0:T(8,128)}, bf16[1792,256]{1,0:T(8,128)(2,1)}, bf16[1792,256]{1,0:T(8,128)(2,1)}, bf16[1792,256]{1,0:T(8,128)(2,1)}) custom-call(bf16[16,8,1792]{2,1,0:T(8,128)(2,1)S(1)} %get-tuple-element.16.ret, bf16[8,8,128]{2,1,0:T(8,128)(2,1)S(1)} %get-tuple-element.17.rret, ...), custom_call_target="tpu_custom_call" | custom-call | tf_op jit(solution)/shard_map/pallas_call | solution.py:562
Async XLA Ops:
  0.6 43.1 %copy-start = (s32[128,8]{0,1:T(8,128)S(1)}, s32[128,8]{0,1:T(8,128)}, u32[]{:S(2)}) copy-start(s32[128,8]{0,1:T(8,128)} %param.9) | copy-start | bytes 12292
  0.6 43.1 %copy-start.1 = (bf16[128,8]{0,1:T(8,128)(2,1)S(1)}, bf16[128,8]{0,1:T(8,128)(2,1)}, u32[]{:S(2)}) copy-start(bf16[128,8]{0,1:T(8,128)(2,1)} %param.10) | copy-start | bytes 6148

commit v4 on v3

--- a/solution.py
+++ b/solution.py
@@ -23,8 +23,8 @@
     tok_hbm, grad_hbm, ids_hbm, rw_hbm, a_hbm, b_hbm, c_hbm,
     ret, rret, sel_ref, ga, gb, gc,
     ids_buf, rw_buf, tokbuf, gradbuf, w3, send1, shard, xs, ys,
-    psx, psy, asx, arx, asy, ary, deltas, hiddens, rp, r1recv, r2send, rsend,
-    in_sem, id_sem, out_sem, s1r, slr, sfr, arr, r1r,
+    psx, psy, asx, arx, asy, ary, deltas, hiddens, rp, r1recv, r2send, midrecv, rsend,
+    in_sem, id_sem, out_sem, s1r, slr, sfr, arr, arl, r1r, mdr,
 ):
     experts = n_ep // SLICES
     stride = ROUTED // experts
@@ -38,7 +38,7 @@
     chunk = 2 * n_dp * CAP
     half = n_dp * CAP
     wab, wc = w3.at[:, pl.ds(0, 2 * hid)], w3.at[:, pl.ds(2 * hid, hid)]
-    w_sem, s1s, sus, sds, sfs, asxs, asys, r1s, r2s, r2r, rts, rtr = (out_sem.at[i] for i in range(12))
+    w_sem, s1s, sus, sds, sfs, asxs, asys, r1s, r2s, r2r, rts, rtr, mds = (out_sem.at[i] for i in range(13))
     g = lax.axis_index("dp")
     e = lax.axis_index("ep")
     hi, lo = e // 2, e % 2
@@ -224,11 +224,16 @@
                 fwd(h, q, c).start()
     pltpu.make_async_copy(w3, w3, w_sem).wait()
 
-    def ar(b, h, part):
+    def half_at(late):
+        return pl.ds(pl.multiple_of((1 - lo if late else lo) * half, PAIR), half)
+
+    def ar(b, k, v, part, late):
+        h = v * per + at_order(k)
         bit = 1 << b
         peer = g + (1 - 2 * ((g // bit) % 2)) * bit
-        src, dst = ((asx, arx), (asy, ary))[part]
-        return rc(src.at[b, h], dst.at[b, h], (asxs, asys)[part], arr.at[b, h, part], dp=peer)
+        src, dst = (r.at[b, h] if late is None else r.at[b, h, half_at(late)] for r in ((asx, arx), (asy, ary))[part])
+        sem = arl.at[b, k - 1, v, part] if late else arr.at[b, h, part]
+        return rc(src, dst, (asxs, asys)[part], sem, dp=peer)
 
     def at_chunk(h):
         return pl.ds(pl.multiple_of(h * chunk, PAIR), chunk)
@@ -236,8 +241,12 @@
     def pair_rows(c):
         return pl.ds(pl.multiple_of(c * PAIR, PAIR), PAIR)
 
-    def r1(h, c):
-        return rc(rp.at[h, 1 - lo, pair_rows(c)], r1recv.at[h, pair_rows(c)], r1s, r1r.at[h, c], ep=other)
+    left = (lw // LANES + 1) // 2 * LANES
+    cols = (pl.ds(0, left), pl.ds(left, lw - left))
+
+    def r1(h, c, m):
+        return rc(rp.at[h, 1 - lo, pair_rows(c), cols[m]], r1recv.at[h, pair_rows(c), cols[m]],
+                  r1s, r1r.at[h, c, m], ep=other)
 
     def over(stage):
         if experts == 1:
@@ -245,8 +254,8 @@
         else:
             lax.fori_loop(0, experts, lambda v, carry: (stage(v), carry)[1], 0)
 
-    def gather_step(s, v):
-        for q in range(2):
+    def gather_step(s, qs, v):
+        for q in qs:
             for ci in range(n_pair):
                 c = pair_at(ci)
                 if s == 1:
@@ -271,23 +280,29 @@
                             @pl.when(jnp.logical_not(inner & ((p == 0) | (p == per - 1))))
                             def _():
                                 fwd(h, q, c).start()
+                        elif s == 2 and q == 0:
+                            @pl.when(jnp.logical_not(inner))
+                            def _():
+                                fwd(h, q, c).start()
                         elif s == 2 or q == 0:
                             fwd(h, q, c).start()
 
-    def cross_far(v):
+    def cross_on(k, q, away, v):
+        h = v * per + at_order(k)
         for ci in range(n_pair):
             c = pair_at(ci)
-
-            @pl.when(inner)
-            def _():
-                h = v * per + at_order(per - 1)
-                fwd_in(h, 1, c).wait_recv()
-                for up in range(2):
-                    @pl.when((pos < per // 2) if up else (pos >= per // 2))
-                    def _():
-                        cross(h, 1, c, up).start()
-
-    def project(k, v):
+            fwd_in(h, q, c).wait_recv()
+            for up in range(2):
+                @pl.when((pos < per // 2) == (up == away))
+                def _():
+                    cross(h, q, c, up).start()
+
+    def rows_in(h, late):
+        if late is None:
+            return at_chunk(h)
+        return pl.ds(pl.multiple_of(h * chunk + (1 - lo if late else lo) * half, PAIR), half)
+
+    def project(k, late, v):
         h = v * per + at_order(k)
 
         def arrived(q):
@@ -295,36 +310,60 @@
                 for ci in range(n_pair):
                     fwd_in(h, q, pair_at(ci)).wait_recv()
 
+            if late is False:
+                return
             if k == 0:
                 pl.when(inner)(wait)
-            elif k == per - 1 and q:
+            elif (k, q) in ((per - 2, 0), (per - 1, 1)):
                 pl.when(jnp.logical_not(inner))(wait)
             else:
                 wait()
 
-        arrived(0)
-        p1 = jnp.dot(xs[at_chunk(h), :], wab[...], preferred_element_type=F32)
-        psx[h] = p1
-        asx[0, h] = p1.astype(BF)
-        ar(0, h, 0).start()
-        arrived(1)
-        p2 = jnp.dot(ys[at_chunk(h), :], wc[...], preferred_element_type=F32)
-        psy[h] = p2
-        asy[0, h] = p2.astype(BF)
-        ar(0, h, 1).start()
-
-    def reduce_step(k, b, v):
+        for part, (rows_of, w, ps, send) in enumerate(((xs, wab, psx, asx), (ys, wc, psy, asy))):
+            arrived(part)
+            p = jnp.dot(rows_of[rows_in(h, late), :], w[...], preferred_element_type=F32)
+            if late is None:
+                ps[h] = p
+                send[0, h] = p.astype(BF)
+            else:
+                ps[h, half_at(late)] = p
+                send[0, h, half_at(late)] = p.astype(BF)
+            ar(0, k, v, part, late).start()
+
+    def reduce_step(k, b, late, v):
         h = v * per + at_order(k)
         for part, (ps, send, recv) in enumerate(((psx, asx, arx), (psy, asy, ary))):
-            ar(b, h, part).wait_recv()
-            s = ps[h] + recv[b, h].astype(F32)
-            ps[h] = s
-            send[b + 1, h] = s.astype(BF)
-            ar(b + 1, h, part).start()
-
-    def finish(k, v):
+            ar(b, k, v, part, late).wait_recv()
+            if late is None:
+                s = ps[h] + recv[b, h].astype(F32)
+                ps[h] = s
+                send[b + 1, h] = s.astype(BF)
+            else:
+                r = half_at(late)
+                s = ps[h, r] + recv[b, h, r].astype(F32)
+                ps[h, r] = s
+                send[b + 1, h, r] = s.astype(BF)
+            ar(b + 1, k, v, part, late).start()
+
+    def start_back(k, m, v):
+        for ci in reversed(range(n_pair)):
+            r1(v * per + at_order(k), pair_at(ci), m).start()
+
+    def to_middle(h, v, m):
+        return rc(rp.at[h, :, :, cols[m]], midrecv.at[v, :, :, cols[m]], mds, mdr.at[v, m],
+                  ep=e + jnp.where(pos < per // 2, 2, -2))
+
+    def merge(v):
+        h = v * per + pos
+        for m, at in enumerate(cols):
+            to_middle(h, v, m).wait_recv()
+            rp[h, :, :, at] = (rp[h, :, :, at].astype(F32) + midrecv[v, :, :, at].astype(F32)).astype(BF)
+            start_back(0, m, v)
+
+    def finish(k, lates, middle, v):
         h = v * per + at_order(k)
-        ar(nb - 1, h, 0).wait_recv()
+        for late in lates:
+            ar(nb - 1, k, v, 0, late).wait_recv()
         s = psx[h] + arx[nb - 1, h].astype(F32)
         gate_pre, up_pre = s[:, :hid], s[:, hid:]
         sig = 1.0 / (1.0 + jnp.exp(-gate_pre))
@@ -332,17 +371,23 @@
         hidden = (sw * up_pre).astype(BF)
         hiddens[at_chunk(h), :] = hidden
         slope = up_pre * sig * (1.0 + gate_pre * (1.0 - sig))
-        ar(nb - 1, h, 1).wait_recv()
+        for late in lates:
+            ar(nb - 1, k, v, 1, late).wait_recv()
         proj = psy[h] + ary[nb - 1, h].astype(F32)
         route = jnp.sum(hidden.astype(F32) * proj, axis=1, keepdims=True)
         d1 = (proj * slope).astype(BF)
         d2 = (proj * sw).astype(BF)
         deltas[at_chunk(h), 0:hid] = d1
         deltas[at_chunk(h), hid:] = d2
-        part = lax.dot_general(
-            jnp.concatenate([d1, d2], axis=1), wab[...], (((1,), (1,)), ((), ())),
-            preferred_element_type=F32)
-        rp[h] = part.reshape(2, half, lw).astype(BF)
+        both = jnp.concatenate([d1, d2], axis=1)
+        for m, at in enumerate(cols):
+            part = lax.dot_general(
+                both, wab[at, :], (((1,), (1,)), ((), ())), preferred_element_type=F32)
+            rp[h, :, :, at] = part.reshape(2, half, part.shape[1]).astype(BF)
+            if middle:
+                to_middle(h, v, m).start()
+            elif k:
+                start_back(k, m, v)
         rsend[h] = jnp.broadcast_to(route, (chunk, LANES)).reshape(2, n_dp, CAP, LANES).astype(BF)
         for l in range(2):
             @pl.when(h * 2 + l != e)
@@ -355,77 +400,54 @@
 
     def send_back(k, v):
         h = v * per + at_order(k)
-        for ci in reversed(range(n_pair)):
-            c = pair_at(ci)
-            r1(h, c).wait_recv()
-            both = rp[h, lo, pair_rows(c)].astype(F32) + r1recv[h, pair_rows(c)].astype(F32)
-            r2send[h, pl.ds(2 * c, 2)] = both.reshape(2, CAP, lw).astype(BF)
-            for b in range(2):
-                gp = 2 * c + b
-
-                def pass_on():
-                    rc(r2send.at[h, gp], ret.at[hi * n_dp + g], r2s, r2r, dp=gp, ep=h * 2 + lo).start()
-
-                def keep():
-                    ret[hi * n_dp + g] = r2send[h, gp]
-
-                if ci or (k and experts == 1):
-                    pass_on()
-                else:
-                    mine = (h == hi) & (gp == g)
-                    pl.when(jnp.logical_not(mine))(pass_on)
-                    pl.when(mine)(keep)
-
-    def G(s):
-        over(functools.partial(gather_step, s))
-
-    def P(k):
-        over(functools.partial(project, k))
-
-    def A(k):
+        for m, at in enumerate(cols):
+            for ci in reversed(range(n_pair)):
+                c = pair_at(ci)
+                r1(h, c, m).wait_recv()
+                both = rp[h, lo, pair_rows(c), at].astype(F32) + r1recv[h, pair_rows(c), at].astype(F32)
+                r2send[h, pl.ds(2 * c, 2), :, at] = both.reshape(2, CAP, both.shape[1]).astype(BF)
+                for b in range(2):
+                    gp = 2 * c + b
+
+                    def pass_on():
+                        rc(r2send.at[h, gp, :, at], ret.at[hi * n_dp + g, :, at], r2s, r2r,
+                           dp=gp, ep=h * 2 + lo).start()
+
+                    def keep():
+                        ret[hi * n_dp + g, :, at] = r2send[h, gp, :, at]
+
+                    if ci or (k and experts == 1):
+                        pass_on()
+                    else:
+                        mine = (h == hi) & (gp == g)
+                        pl.when(jnp.logical_not(mine))(pass_on)
+                        pl.when(mine)(keep)
+
+    def G(s, *qs):
+        over(functools.partial(gather_step, s, qs))
+
+    def X(k, q, away):
+        over(functools.partial(cross_on, k, q, away))
+
+    def P(k, late=None):
+        over(functools.partial(project, k, late))
+
+    def A(k, late=None):
         for b in range(nb - 1):
-            over(functools.partial(reduce_step, k, b))
-
-    def F(k):
-        over(functools.partial(finish, k))
-
-    def S(k):
-        def start(v):
-            for ci in reversed(range(n_pair)):
-                r1(v * per + at_order(k), pair_at(ci)).start()
-
-        over(start)
+            over(functools.partial(reduce_step, k, b, late))
+
+    def F(k, *lates, middle=False):
+        over(functools.partial(finish, k, lates or (None,), middle))
+
+    def S(k, *parts):
+        for m in parts:
+            over(functools.partial(start_back, k, m))
 
     def R(k):
         over(functools.partial(send_back, k))
 
-    G(1)
-    P(0)
-    A(0)
-    G(2)
-    P(1)
-    A(1)
-    F(0)
-    pl.when(inner)(functools.partial(S, 0))
-    G(3)
-    P(2)
-    over(cross_far)
-    A(2)
-    F(1)
-    S(1)
-    P(3)
-    A(3)
-    F(2)
-    S(2)
-    R(1)
-    F(3)
-    S(3)
-    pl.when(jnp.logical_not(inner))(functools.partial(S, 0))
-    R(2)
-    R(3)
-    R(0)
-
     tile = 256 if lw % 256 == 0 else 128
+    tiles = lw // tile
 
     def wgrad(i, carry):
         ds = pl.ds(pl.multiple_of(i * tile, LANES), tile)
@@ -436,29 +458,107 @@
         gc[ds, :] = lax.dot_general(ys[:, ds], hiddens[...], dn, preferred_element_type=F32).astype(BF)
         return carry
 
-    lax.fori_loop(0, lw // tile, wgrad, 0)
+    def W(part):
+        lax.fori_loop((0, (tiles + 1) // 2)[part], ((tiles + 1) // 2, tiles)[part], wgrad, 0)
+
+    G(1, 0, 1)
+    P(0)
+    A(0)
+
+    @pl.when(inner)
+    def _():
+        P(1, False)
+        G(2, 0)
+        A(1, False)
+        X(2, 0, 0)
+        P(1, True)
+        G(2, 1)
+        F(0)
+        A(1, True)
+        P(3, False)
+        P(2)
+        A(3, False)
+        X(3, 1, 1)
+        P(3, True)
+        A(3, True)
+        F(1, False, True, middle=True)
+        A(2)
+        F(3, False, True)
+        F(2)
+        R(3)
+        over(merge)
+        W(0)
+        R(2)
+        W(1)
+        R(0)
+
+    @pl.when(jnp.logical_not(inner))
+    def _():
+        G(2, 0, 1)
+        P(1)
+        A(1)
+        F(0)
+        G(3, 0)
+        P(2, False)
+        A(2, False)
+        P(2, True)
+        G(3, 1)
+        S(0, 0)
+        P(3, False)
+        A(2, True)
+        F(1)
+        A(3, False)
+        P(3, True)
+        A(3, True)
+        F(2, False, True)
+        R(1)
+        F(3, False, True)
+        W(0)
+        R(2)
+        S(0, 1)
+        R(3)
+        R(0)
+        W(1)
 
     def settle(ref, sem):
         pltpu.make_async_copy(ref, ref, sem).wait()
 
-    back, routes = ret.at[pl.ds(0, n_hi * n_dp - 1)], rret.at[pl.ds(0, n_ep - 1)]
-    settle(back, r2r)
+    def settle_back(sem):
+        for group, fewer in ((inner, experts * n_dp), (jnp.logical_not(inner), 0)):
+            @pl.when(group)
+            def _():
+                settle(ret.at[pl.ds(0, n_hi * n_dp - 1 - fewer)], sem)
+
+    routes = rret.at[pl.ds(0, n_ep - 1)]
+    settle_back(r2r)
     settle(routes, rtr)
-    settle(back, r2s)
+    settle_back(r2s)
     settle(routes, rts)
-    settle(r1recv, r1s)
+
+    @pl.when(inner)
+    def _():
+        settle(r1recv.at[pl.ds(0, n_hi - experts)], r1s)
+        settle(midrecv, mds)
+        for w in range(experts):
+            unused = (w * per + per - 1 - pos) * n_dp
+            ret[pl.ds(unused, n_dp)] = jnp.zeros((n_dp, CAP, lw), BF)
+
+    @pl.when(jnp.logical_not(inner))
+    def _():
+        settle(r1recv, r1s)
+
     settle(asx, asxs)
     settle(asy, asys)
     settle(xs.at[pl.ds(0, PAIR * (n_dp * experts - 1)), :], s1s)
     K = 2 * n_pair
     for at in range(per):
         ends = at in (0, per - 1)
-        crossing = {0: K, per - 2: n_pair}
         down = per - 1 - at
+        crossing = lambda behind: n_pair if behind else K
         sent = (
-            (sus, (at + 1) * K + crossing.get(at, 0) if down else 0),
-            (sds, (down + 1) * K + crossing.get(down, 0) if at else 0),
-            (sfs, (per - 1) * K + (n_pair if ends else 0)),
+            (sus, (at + 1) * K + crossing(at) if down else 0),
+            (sds, (down + 1) * K + crossing(down) if at else 0),
+            (sfs, (per - 1 if ends else per - 2) * K + n_pair),
         )
 
         @pl.when(pos == at)
@@ -520,7 +620,7 @@
     n_dp, n_ep = lax.axis_size("dp"), lax.axis_size("ep")
     experts = n_ep // SLICES
     n_hi = n_ep // 2
-    n_pair = n_dp // 2
+    n_pair, per = n_dp // 2, SLICES // 2
     rows, width = tokens.shape
     lw, hid = gate_matrix.shape
     nb = n_dp.bit_length() - 1
@@ -552,8 +652,9 @@
             V((nb, n_hi, chunk, hid), BF), V((nb, n_hi, chunk, hid), BF),
             V((total, 2 * hid), BF), V((total, hid), BF),
             V((n_hi, 2, half, lw), BF), V((n_hi, half, lw), BF), V((n_hi, n_dp, CAP, lw), BF),
+            V((experts, 2, half, lw), BF),
             V((n_hi, 2, n_dp, CAP, LANES), BF),
-            D(2, n_dp), D(2), D(12), D(2, experts, n_dp), D(n_hi, K), D(n_hi, K), D(nb, n_hi, 2), D(n_hi, n_pair),
+            D(2, n_dp), D(2), D(13), D(2, experts, n_dp), D(n_hi, K), D(n_hi, K), D(nb, n_hi, 2), D(nb, per - 1, experts, 2), D(n_hi, n_pair, 2), D(experts, 2),
         ],
         compiler_params=pltpu.CompilerParams(
             collective_id=0, has_side_effects=True, vmem_limit_bytes=VMEM_BYTES),

time: 46.7 us -> 45.4 us (0.972)
  Pallas kernels: 45.8 us -> 44.5 us
    pallas_call x1, Pallas kernels: 43.1 us -> 41.7 us  [body(): pl.pallas_call(functools.partial(kernel, n_dp, n_ep), out_shape=(V((n_hi...]
where the time goes in v4:
time: 45.4 us; the launch traced here: 45.2 us
  Pallas kernels  44.5 us (98%)
  between operations  0.67 us (1%)
    pallas_call x1, Pallas kernels, body(): pl.pallas_call(functools.partial(kernel, n_dp, n_ep), out_shape=(V((n_hi...  41.7 us
    pallas_call x1, Pallas kernels, body(): pl.pallas_call(finish_kernel, out_shape=(jax.ShapeDtypeStruct((rows, widt...  2.79 us

profile of v4, /device:TPU:0, one launch (start us, length us, event | category | flops | bytes accessed | tf_op | source)
XLA Modules:
  0.0 45.2 jit_solution(4609754194272258470)
XLA Ops:
  0.6 0.0 copy-start
  0.6 0.0 copy-start.1
  0.7 41.7 %shard_map.110 = (bf16[16,8,1792]{2,1,0:T(8,128)(2,1)S(1)}, bf16[8,8,128]{2,1,0:T(8,128)(2,1)S(1)}, f32[8,128]{1,0:T(8,128)S(1)}, bf16[1792,256]{1,0:T(8,128)(2,...) custom-call(bf16[128,7168]{1,0:T(8,128)(2,1)} %tok_hbm.1, bf16[128,7168]{1,0:T(8,128)(2,1)} %grad_hbm.1, ...), custom_call_target="tpu_custom_call" | custom-call | tf_op jit(solution)/shard_map/pallas_call | solution.py:637
  42.4 0.0 copy-done
  42.4 0.0 copy-done.1
  42.4 2.8 %shard_map.111 = (bf16[128,7168]{1,0:T(8,128)(2,1)}, f32[8,128]{1,0:T(8,128)}, bf16[1792,256]{1,0:T(8,128)(2,1)}, bf16[1792,256]{1,0:T(8,128)(2,1)}, bf16[1792,256]{1,0:T(8,128)(2,1)}) custom-call(bf16[16,8,1792]{2,1,0:T(8,128)(2,1)S(1)} %get-tuple-element.16.ret, bf16[8,8,128]{2,1,0:T(8,128)(2,1)S(1)} %get-tuple-element.17.rret, ...), custom_call_target="tpu_custom_call" | custom-call | tf_op jit(solution)/shard_map/pallas_call | solution.py:663
Async XLA Ops:
  0.6 41.8 %copy-start = (s32[128,8]{0,1:T(8,128)S(1)}, s32[128,8]{0,1:T(8,128)}, u32[]{:S(2)}) copy-start(s32[128,8]{0,1:T(8,128)} %param.9) | copy-start | bytes 12292
  0.6 41.8 %copy-start.1 = (bf16[128,8]{0,1:T(8,128)(2,1)S(1)}, bf16[128,8]{0,1:T(8,128)(2,1)}, u32[]{:S(2)}) copy-start(bf16[128,8]{0,1:T(8,128)(2,1)} %param.10) | copy-start | bytes 6148

commit v5 on v4

--- a/solution.py
+++ b/solution.py
@@ -70,7 +70,7 @@
     ]
     for c in id_copies:
         c.start()
-    order = list(range(1, n_dp)) + [0]
+    order = list(range(2, n_dp)) + [1, 0]
     loads = []
     for q, (src, buf) in enumerate(((tok_hbm, tokbuf), (grad_hbm, gradbuf))):
         for j in order:

time: 45.4 us -> 45.4 us (level)
  no operation moved by 1% of the time
where the time goes in v5:
time: 45.4 us; the launch traced here: 45.3 us
  Pallas kernels  44.6 us (98%)
  between operations  0.67 us (1%)
    pallas_call x1, Pallas kernels, body(): pl.pallas_call(functools.partial(kernel, n_dp, n_ep), out_shape=(V((n_hi...  41.8 us
    pallas_call x1, Pallas kernels, body(): pl.pallas_call(finish_kernel, out_shape=(jax.ShapeDtypeStruct((rows, widt...  2.79 us

profile of v5, /device:TPU:0, one launch (start us, length us, event | category | flops | bytes accessed | tf_op | source)
XLA Modules:
  0.0 45.3 jit_solution(6460166985830792399)
XLA Ops:
  0.6 0.0 copy-start
  0.6 0.0 copy-start.1
  0.7 41.8 %shard_map.110 = (bf16[16,8,1792]{2,1,0:T(8,128)(2,1)S(1)}, bf16[8,8,128]{2,1,0:T(8,128)(2,1)S(1)}, f32[8,128]{1,0:T(8,128)S(1)}, bf16[1792,256]{1,0:T(8,128)(2,...) custom-call(bf16[128,7168]{1,0:T(8,128)(2,1)} %tok_hbm.1, bf16[128,7168]{1,0:T(8,128)(2,1)} %grad_hbm.1, ...), custom_call_target="tpu_custom_call" | custom-call | tf_op jit(solution)/shard_map/pallas_call | solution.py:637
  42.5 0.0 copy-done
  42.5 0.0 copy-done.1
  42.5 2.8 %shard_map.111 = (bf16[128,7168]{1,0:T(8,128)(2,1)}, f32[8,128]{1,0:T(8,128)}, bf16[1792,256]{1,0:T(8,128)(2,1)}, bf16[1792,256]{1,0:T(8,128)(2,1)}, bf16[1792,256]{1,0:T(8,128)(2,1)}) custom-call(bf16[16,8,1792]{2,1,0:T(8,128)(2,1)S(1)} %get-tuple-element.16.ret, bf16[8,8,128]{2,1,0:T(8,128)(2,1)S(1)} %get-tuple-element.17.rret, ...), custom_call_target="tpu_custom_call" | custom-call | tf_op jit(solution)/shard_map/pallas_call | solution.py:663
Async XLA Ops:
  0.6 41.8 %copy-start = (s32[128,8]{0,1:T(8,128)S(1)}, s32[128,8]{0,1:T(8,128)}, u32[]{:S(2)}) copy-start(s32[128,8]{0,1:T(8,128)} %param.9) | copy-start | bytes 12292
  0.6 41.8 %copy-start.1 = (bf16[128,8]{0,1:T(8,128)(2,1)S(1)}, bf16[128,8]{0,1:T(8,128)(2,1)}, u32[]{:S(2)}) copy-start(bf16[128,8]{0,1:T(8,128)(2,1)} %param.10) | copy-start | bytes 6148
